TPU v7x, 32 devices: a 4x4x1 block of a 4x4x8 slice. The times are simulated.
32 devices in a mesh: batch: 1 (over z), rows: 4 (over y), ksplit: 8 (over x, core).
Axes of the slice: x: 4, y: 4, z: 1, core: 2. Of those that a mesh axis runs over, the one named last changes fastest.
The devices are a block of a 4x4x8 slice.
Arguments:
- a_vals: bfloat16 [4, 8, 16, 128, 128], P(('batch', 'rows'), 'ksplit')
- b_vals: bfloat16 [8, 64, 128, 128], P(('batch', 'ksplit'))
- pairs: int32 [4, 8, 512, 1, 2], P(('batch', 'rows'), 'ksplit')
- plist_idx: int32 [4, 8, 512, 2], P(('batch', 'rows'), 'ksplit')
- c_idx: int32 [4, 8, 64, 2], P(('batch', 'rows'), 'ksplit')
Outputs:
- output: float32 [4, 8, 64, 128, 128], P(('batch', 'rows'), 'ksplit')
All inputs are finite; a program needn't handle non-finite values.
Results may differ from a plain program's by a relative error of at most 0.001.
Values are sent between devices in bfloat16 or wider.
A program may use at most 768 MiB of HBM per device.

v0:
```python
import jax
import jax.numpy as jnp
from jax import lax
from jax.sharding import PartitionSpec as P


def solution(mesh):
    row_spec = P(('batch', 'rows'), 'ksplit')
    col_spec = P(('batch', 'ksplit'))

    def device_step(a_loc, b_loc, pair_loc, plist_loc, cidx_loc):
        a_blocks = a_loc[0, 0]
        b_blocks = b_loc[0]
        pair_tab = pair_loc[0, 0]
        own_idx = cidx_loc[0, 0]
        block_size = a_blocks.shape[-1]
        a_sel = jnp.take(a_blocks, pair_tab[:, :, 0], axis=0)
        b_sel = jnp.take(b_blocks, pair_tab[:, :, 1], axis=0)
        part_sums = jnp.einsum('stab,stbc->sac', a_sel, b_sel, preferred_element_type=jnp.float32).astype(jnp.bfloat16)
        recv_vals = lax.all_to_all(part_sums, 'ksplit', 0, 0, tiled=True)
        recv_idx = lax.all_to_all(plist_loc[0, 0], 'ksplit', 0, 0, tiled=True)
        hit_mask = jnp.all(own_idx[:, None, :] == recv_idx[None, :, :], axis=-1).astype(jnp.bfloat16)
        flat_vals = recv_vals.reshape(recv_vals.shape[0], block_size * block_size)
        c_flat = jnp.dot(hit_mask, flat_vals, preferred_element_type=jnp.float32)
        return c_flat.reshape(1, 1, own_idx.shape[0], block_size, block_size)

    return jax.shard_map(device_step, mesh=mesh, in_specs=(row_spec, col_spec, row_spec, row_spec, row_spec), out_specs=row_spec, check_vma=False)
```

profile of v0, /device:TPU:97, one launch (start us, length us, event | category | flops | bytes accessed | tf_op | source)
XLA Modules:
  0.0 304.4 jit_solution(13830330489369672932)
XLA Ops:
  0.0 0.0 copy-start
  0.0 0.9 all_to_all.9
  0.9 0.7 reshape.91
  1.6 6.0 %all-to-all-start = ((s32[8,1,128]{2,1,0:T(1,128)}), s32[8,1,128]{2,1,0:T(1,128)S(1)}, u32[]{:S(2)}, u32[]{:S(2)}) async-start(s32[8,1,128]{2,1,0:T(1,128)} %reshape.91), calls=%async_computation | async-start | bytes 8192 | tf_op jit(solution)/shard_map/all_to_all | solution.py:21
  7.6 0.8 and_reduce_fusion.1
  8.4 14.8 %gather_fusion = bf16[512,128,128]{2,1,0:T(8,128)(2,1)} fusion(bf16[16,128,128]{2,1,0:T(8,128)(2,1)} %bitcast.29, s32[1024]{0:T(1024)S(1)} %pad_clamp_fusion.1), kind=kCustom, calls=%fused_computation | custom fusion | bytes 33556480 | tf_op jit(solution)/shard_map/jit(_take)/gather | solution.py:17
  23.3 0.0 copy-done
  23.3 13.9 %gather_fusion.1 = bf16[512,128,128]{2,1,0:T(8,128)(2,1)} fusion(bf16[64,128,128]{2,1,0:T(8,128)(2,1)S(1)} %bitcast.28, s32[1024]{0:T(1024)S(1)} %pad_clamp_fusion), kind=kCustom, calls=%fused_computation.1 | custom fusion | bytes 33556480 | tf_op jit(solution)/shard_map/jit(_take)/gather | solution.py:18
  37.2 18.8 %fusion.5 = bf16[512,128,128]{2,1,0:T(8,128)(2,1)} fusion(bf16[512,128,128]{2,1,0:T(8,128)(2,1)} %gather_fusion.1, pred[512]{0:T(512)(128)(4,1)S(1)} %get-tuple-element.9, bf16[512,128,128]{2,1,0:T(8,128)(2,1)} %gather_fusion, pred[512]{0:T(512)(128)(4,1)S(1)} %get-tuple-element.5), kind=kOutput, calls=%fused_computation.8 | convolution fusion | flops 2172649472 | bytes 50332672 | tf_op jit(solution)/shard_map/stab,stbc->sac/dot_general | solution.py:19
  55.9 0.0 copy-start.2
  55.9 0.0 all-to-all-done
  55.9 6.1 %all-to-all-start.1 = ((bf16[512,128,128]{2,1,0:T(8,128)(2,1)}), bf16[512,128,128]{2,1,0:T(8,128)(2,1)}, u32[]{:S(2)}, u32[]{:S(2)}) async-start(bf16[512,128,128]{2,1,0:T(8,128)(2,1)} %fusion.5), calls=%async_computation.1 | async-start | bytes 33554432 | tf_op jit(solution)/shard_map/all_to_all | solution.py:20
  62.0 0.5 broadcast.60
  62.5 0.7 reduce.4
  63.2 0.1 reshape.92
  63.3 0.1 eq.19
  63.4 0.0 copy-done.2
  63.4 0.1 compare_reduce_fusion
  63.5 181.7 %all-to-all-done.1 = bf16[512,128,128]{2,1,0:T(8,128)(2,1)} async-done(((bf16[512,128,128]{2,1,0:T(8,128)(2,1)}), bf16[512,128,128]{2,1,0:T(8,128)(2,1)}, u32[]{:S(2)}, u32[]{:S(2)}) %all-to-all-start.1) | async-done | bytes 16777248 | tf_op jit(solution)/shard_map/all_to_all | solution.py:20
  245.2 19.4 %copy.26 = bf16[64,8,128,128]{3,1,2,0:T(8,128)(2,1)} copy(bf16[64,8,128,128]{3,2,1,0:T(8,128)(2,1)} %bitcast.12) | data formatting | bytes 33554432
  264.6 22.6 %copy.21 = bf16[16384,512]{1,0:T(8,128)(2,1)} copy(bf16[16384,512]{0,1:T(8,128)(2,1)} %bitcast.31) | data formatting | bytes 33554432 | tf_op jit(solution)/shard_map/dot_general | solution.py:24
  287.2 10.6 %convolution_bitcast_fusion = f32[1,1,64,128,128]{4,2,3,1,0:T(8,128)} fusion(bf16[128,128,512]{2,1,0:T(8,128)(2,1)} %bitcast.30, pred[64,512]{1,0:T(8,128)(4,1)S(1)} %compare_reduce_fusion), kind=kOutput, calls=%fused_computation.10 | convolution fusion | flops 1073741824 | bytes 21004288 | tf_op jit(solution)/shard_map/dot_general | solution.py:24
  297.8 6.6 %copy.22 = f32[1,1,64,128,128]{4,3,2,1,0:T(8,128)} copy(f32[1,1,64,128,128]{4,2,3,1,0:T(8,128)} %convolution_bitcast_fusion) | data formatting | bytes 8388608 | tf_op jit(solution)/shard_map/dot_general | solution.py:24
  304.4 0.0 copy-done.1
  (5 shorter events, 0.0 us)
Async XLA Ops:
  0.0 23.3 %copy-start = (bf16[1,64,128,128]{3,2,1,0:T(8,128)(2,1)S(1)}, bf16[1,64,128,128]{3,2,1,0:T(8,128)(2,1)}, u32[]{:S(2)}) copy-start(bf16[1,64,128,128]{3,2,1,0:T(8,128)(2,1)} %param.6) | copy-start | bytes 6291460
  1.6 54.3 %all-to-all-start = ((s32[8,1,128]{2,1,0:T(1,128)}), s32[8,1,128]{2,1,0:T(1,128)S(1)}, u32[]{:S(2)}, u32[]{:S(2)}) async-start(s32[8,1,128]{2,1,0:T(1,128)} %reshape.91), calls=%async_computation | async-start | bytes 8192 | tf_op jit(solution)/shard_map/all_to_all | solution.py:21
  55.9 7.4 %copy-start.2 = (s32[1,1,64,2]{2,3,1,0:T(2,128)S(1)}, s32[1,1,64,2]{2,3,1,0:T(2,128)}, u32[]{:S(2)}) copy-start(s32[1,1,64,2]{2,3,1,0:T(2,128)} %param.9) | copy-start | bytes 1540
  55.9 189.2 %all-to-all-start.1 = ((bf16[512,128,128]{2,1,0:T(8,128)(2,1)}), bf16[512,128,128]{2,1,0:T(8,128)(2,1)}, u32[]{:S(2)}, u32[]{:S(2)}) async-start(bf16[512,128,128]{2,1,0:T(8,128)(2,1)} %fusion.5), calls=%async_computation.1 | async-start | bytes 33554432 | tf_op jit(solution)/shard_map/all_to_all | solution.py:20
  264.6 39.8 %copy-start.1 = (bf16[1,64,128,128]{3,2,1,0:T(8,128)(2,1)S(1)}, bf16[1,64,128,128]{3,2,1,0:T(8,128)(2,1)}, u32[]{:S(2)}) copy-start(bf16[1,64,128,128]{3,2,1,0:T(8,128)(2,1)} %param.6) | copy-start | bytes 6291460
where the time goes:
time: 305 us; the launch traced here: 304 us
  waiting for transfers between devices  182 us (60%)
  local copies, waits for them, and re-layouts  79.7 us (26%)
  matrix products  29.3 us (10%)
  starting transfers between devices  12.1 us (4%)
    all_to_all x1, waiting for transfers between devices, device_step(): recv_vals = lax.all_to_all(part_sums, 'ksplit', 0, 0, tiled=True)  182 us
    dot_general x2, local copies, waits for them, and re-layouts, device_step(): c_flat = jnp.dot(hit_mask, flat_vals, preferred_element_type=jnp.float32)  29.2 us
    unnamed x9, local copies, waits for them, and re-layouts  20.2 us
    dot_general x1, matrix products, device_step(): jnp.einsum('stab,stbc->sac', a_sel, b_sel, preferred_element_type=jnp.flo...  18.8 us
    gather x1, local copies, waits for them, and re-layouts, device_step(): a_sel = jnp.take(a_blocks, pair_tab[:, :, 0], axis=0)  14.8 us
    gather x1, local copies, waits for them, and re-layouts, device_step(): b_sel = jnp.take(b_blocks, pair_tab[:, :, 1], axis=0)  13.9 us
    dot_general x1, matrix products, device_step(): c_flat = jnp.dot(hit_mask, flat_vals, preferred_element_type=jnp.float32)  10.6 us
  transfers between devices with their start and end apart: 2, of which 1 were waited for; matrix products, arithmetic and copies ran while one was open for 16% of the time, Pallas kernels for 0%

commit v1 on v0

v1 whole, which is shorter than its diff:
```python
import functools

import jax
import jax.numpy as jnp
from jax import lax
from jax.experimental import pallas as pl
from jax.experimental.pallas import tpu as pltpu
from jax.sharding import PartitionSpec as P

MESH = pl.DeviceIdType.MESH
HALF_SET = 32
CHUNK = 4
UNROLL = 8
FRONT = 8


class Move:
    def __init__(self, link, kind, src, dst, part, first, count, dep):
        self.link, self.kind, self.src, self.dst = link, kind, src, dst
        self.part, self.first, self.count, self.dep = part, first, count, dep
        self.after = []
        self.shift = 0
        self.arrive = None


def cut(first, count, size):
    return [(first + at, min(size, count - at)) for at in range(0, count, size)]


def plan(n_a, n_b, half_set):
    half = half_set // 2
    quarter = (n_b - half_set) // 4
    h1, h2 = cut(0, half // 2, CHUNK), cut(half // 2, half - half // 2, CHUNK)
    q1, q2 = cut(0, quarter // 2, CHUNK), cut(quarter // 2, quarter - quarter // 2, CHUNK)
    a1, a2 = (0, n_a // 2), (n_a // 2, n_a - n_a // 2)
    moves = []

    def add(link, kind, src, dst, part, piece, dep, shift=0):
        move = Move(link, kind, src, dst, part, piece[0], piece[1], dep)
        move.shift = shift
        move.index = len(moves)
        moves.append(move)
        if dep is not None:
            dep.after.append(move)
        if link != "d":
            add_pair(move)
        return move

    def add_pair(move):
        row = {"+y": -1, "-y": 1}.get(move.link, 0) + move.shift
        add("d", move.kind, move.dst, move.dst, move.part, (move.first, move.count), move, row)

    def spread(move, up, down, piece):
        for link in ("+y",) * up + ("-y",) * down:
            step = 1 if link == "+y" else -1
            nxt = add(link, "b", move.dst, move.dst, move.part, piece, move)
            if move.part == "q":
                if (link == "+y" and piece in q1) or (link == "-y" and piece in q2):
                    add(link, "b", move.dst, move.dst, "q", piece, nxt, -step)

    def over_x(link, back, pieces, part, group):
        out = []
        for piece in pieces:
            move = add(link, "b", 0, back, part, piece, None)
            out.append((move, piece, group))
        return out

    add("d", "b", 0, 0, "all", (0, n_b), None)
    add("d", "a", 0, 0, "all", (0, n_a), None)
    right = over_x("+x", 3, h1, "h", 1) + over_x("+x", 3, h2, "h", 2) + over_x("+x", 3, q1, "q", 1) + over_x("+x", 3, q2, "q", 2)
    left = over_x("-x", 1, h2, "h", 2) + over_x("-x", 1, h1, "h", 1) + over_x("-x", 1, q2, "q", 2) + over_x("-x", 1, q1, "q", 1)
    for received, link, keep in ((right, "+x", 1), (left, "-x", 2)):
        for move, piece, group in received:
            spread(move, move.part == "q" or group == 1, move.part == "q" or group == 2, piece)
            if group == keep:
                nxt = add(link, "b", move.dst, 2, move.part, piece, move)
                spread(nxt, nxt.part == "q" or group == 1, nxt.part == "q" or group == 2, piece)
    late = []
    for (received, link, back, half_a) in ((right, "+x", 3, a1), (left, "-x", 1, a2)):
        for piece in (a1, a2) if link == "+x" else (a2, a1):
            move = add(link, "a", 0, back, "all", piece, received[-1][0])
            if piece == half_a:
                add(link, "a", move.dst, 2, "all", piece, move)
    return moves


def expected(moves):
    free = {"+x": 0.0, "-x": 0.0, "+y": 0.0, "-y": 0.0, "d": 0.0}
    lag = {"+x": 2.6, "-x": 2.6, "+y": 2.6, "-y": 2.6, "d": 1.4}
    ready = [(0.0, i, m) for i, m in enumerate(moves) if m.dep is None]
    order = []
    count = len(moves)
    while ready:
        ready.sort(key=lambda item: (item[0], item[1]))
        at, _, move = ready.pop(0)
        begin = max(at, free[move.link])
        free[move.link] = begin + move.count * (0.1 if move.link == "d" else 1.0)
        move.arrive = free[move.link] + lag[move.link]
        order.append(move)
        for nxt in move.after:
            ready.append((move.arrive, nxt.index, nxt))
    assert len(order) == count
    return sorted(moves, key=lambda m: (m.arrive, m.index))


def kernel(sizes, a_hbm, b_hbm, pairs_hbm, plist_hbm, own_hbm, out_hbm, *scratch):
    n_x, n_y, n_a, n_b, n_own = sizes
    a_slot, b_slot = scratch[0:8], scratch[8:16]
    (acc, pairs_own, plist_own, own, pairs_in, plist_in, table_v, table,
     send_sem, recv_sem, list_send, list_recv, load_sem, out_sem) = scratch[16:]
    y = lax.axis_index("rows")
    p = lax.axis_index("ksplit")
    x, core = p // 2, p % 2
    moves = plan(n_a, n_b, HALF_SET)
    arrivals = expected(moves)

    def at(dx, other):
        return 2 * ((x + dx) % n_x) + (core + other) % 2

    target = {
        "+x": {"ksplit": at(1, 0)},
        "-x": {"ksplit": at(n_x - 1, 0)},
        "+y": {"rows": (y + 1) % n_y},
        "-y": {"rows": (y + n_y - 1) % n_y},
        "d": {"ksplit": at(0, 1)},
    }

    loads = [
        pltpu.make_async_copy(b_hbm, b_slot[0], load_sem.at[0]),
        pltpu.make_async_copy(a_hbm, a_slot[0], load_sem.at[1]),
        pltpu.make_async_copy(pairs_hbm, pairs_own, load_sem.at[2]),
        pltpu.make_async_copy(plist_hbm, plist_own, load_sem.at[3]),
        pltpu.make_async_copy(own_hbm, own, load_sem.at[4]),
    ]
    for load in loads:
        load.start()

    peers = [(dx, other) for dx in range(n_x) for other in range(2) if (dx, other) != (0, 0)]
    barrier = pltpu.get_barrier_semaphore()
    for dx, other in peers:
        pl.semaphore_signal(barrier, inc=1, device_id={"ksplit": at(dx, other)}, device_id_type=MESH)
    for link in ("+y", "-y"):
        pl.semaphore_signal(barrier, inc=1, device_id=target[link], device_id_type=MESH)
    pl.semaphore_wait(barrier, len(peers) + 2)

    def copy(move, row):
        holder = (row + move.shift + 2 * n_y) % n_y
        half = HALF_SET // 2
        quarter = (n_b - HALF_SET) // 4
        base = {"all": 0, "h": (holder % 2) * half, "q": HALF_SET + holder * quarter}[move.part]
        where = pl.ds(base + move.first, move.count)
        slots = a_slot if move.kind == "a" else b_slot
        src = slots[2 * move.src]
        dst = slots[2 * move.dst + (1 if move.link == "d" else 0)]
        return pltpu.make_async_remote_copy(
            src_ref=src.at[where],
            dst_ref=dst.at[where],
            send_sem=send_sem.at[move.index],
            recv_sem=recv_sem.at[move.index],
            device_id=target[move.link],
            device_id_type=MESH,
        )

    def start(move):
        copy(move, y).start()

    def receive(move):
        row = {"+y": y + n_y - 1, "-y": y + 1}.get(move.link, y)
        copy(move, row).wait_recv()

    def lists(number, dx, other):
        mine, theirs = 2 * dx + other, 2 * ((n_x - dx) % n_x) + other
        where = pl.ds(pl.multiple_of(((x + dx) % n_x) * 128, 128), 128)
        pair = []
        for which, (src, dst) in enumerate(((pairs_own, pairs_in), (plist_own, plist_in))):
            pair.append(pltpu.make_async_remote_copy(
                src_ref=src.at[:, where],
                dst_ref=dst.at[theirs],
                send_sem=list_send.at[2 * number + which],
                recv_sem=list_recv.at[2 * number + which],
                device_id={"ksplit": at(dx, other)},
                device_id_type=MESH,
            ))
        return pair

    def lists_in(number, dx, other):
        mine = 2 * dx + other
        pair = []
        back = peers.index(((n_x - dx) % n_x, other))
        for which, (src, dst) in enumerate(((pairs_own, pairs_in), (plist_own, plist_in))):
            pair.append(pltpu.make_async_remote_copy(
                src_ref=src.at[:, pl.ds(0, 128)],
                dst_ref=dst.at[mine],
                send_sem=list_send.at[2 * back + which],
                recv_sem=list_recv.at[2 * back + which],
                device_id={"ksplit": at(dx, other)},
                device_id_type=MESH,
            ))
        return pair

    loads[0].wait()
    for move in moves:
        if move.dep is None and move.kind == "b" and move.link != "d":
            start(move)
    for load in loads[1:]:
        load.wait()
    for number, (dx, other) in enumerate(peers):
        for one in lists(number, dx, other):
            one.start()
    for move in moves:
        if move.dep is None and (move.kind == "a" or move.link == "d"):
            start(move)

    def make_table():
        mine = pl.ds(pl.multiple_of(x * 128, 128), 128)
        pairs_in[0] = pairs_own[:, mine]
        plist_in[0] = plist_own[:, mine]
        for number, (dx, other) in enumerate(peers):
            for one in lists_in(number, dx, other):
                one.wait_recv()
        key = plist_in[:, 0, :] * 65536 + plist_in[:, 1, :]
        code = pairs_in[:, 0, :] * 65536 + pairs_in[:, 1, :]
        wanted = own[0:1, :] * 65536 + own[1:2, :]
        wanted = jnp.concatenate([wanted] * (128 // n_own), axis=1)
        wanted = jnp.broadcast_to(wanted, key.shape)

        def turn(_, state):
            key, code, found = state
            found = jnp.where(key == wanted, code, found)
            return pltpu.roll(key, 1, 1), pltpu.roll(code, 1, 1), found

        _, _, found = lax.fori_loop(0, 128, turn, (key, code, jnp.zeros_like(code)), unroll=8)
        table_v[0] = found // 65536
        table_v[1] = found % 65536

    def use_table():
        to_smem = pltpu.make_async_copy(table_v, table, load_sem.at[5])
        to_smem.start()
        to_smem.wait()

    def product(slot, c):
        left = a_slot[slot][table[0, slot, c]]
        right = b_slot[slot][table[1, slot, c]]
        part = jnp.dot(left, right, preferred_element_type=jnp.float32)
        return part.astype(jnp.bfloat16).astype(jnp.float32)

    def compute(slots, first=False, last=False):
        def step(i, _):
            for u in range(UNROLL):
                c = i * UNROLL + u
                total = product(slots[0], c)
                for slot in slots[1:]:
                    total = total + product(slot, c)
                acc[c] = total if first else acc[c] + total
            if last:
                out_copy(i).start()
            return 0

        lax.fori_loop(0, n_own // UNROLL, step, 0)

    def out_copy(i):
        where = pl.ds(i * UNROLL, UNROLL)
        return pltpu.make_async_copy(acc.at[where], out_hbm.at[where], out_sem.at[i])

    seen = set()

    def take(move):
        if move.index not in seen:
            seen.add(move.index)
            receive(move)
            for nxt in move.after:
                start(nxt)

    def need(dx, other):
        return [m for m in arrivals if m.dst == dx and (m.link == "d") == bool(other)]

    wire = [m for m in arrivals if m.link != "d"]
    early = [m for m in wire if m.arrive < 10.0]
    for move in early:
        take(move)
    make_table()
    for move in wire:
        if move.arrive < 14.0:
            take(move)
    use_table()
    for move in need(0, 1):
        take(move)
    compute((0, 1), first=True)
    done = {0}
    for position, move in enumerate(wire):
        take(move)
        rest = [m for m in wire[position + 1:]]
        for dx in (3, 1):
            if dx not in done and not [m for m in rest if m.dst == dx]:
                done.add(dx)
                for m in need(dx, 1):
                    take(m)
                compute((2 * dx, 2 * dx + 1))
    compute((4,))
    for m in need(2, 1):
        take(m)
    compute((5,), last=True)
    assert len(seen) == len(moves)

    for number, (dx, other) in enumerate(peers):
        for one in lists(number, dx, other):
            one.wait_send()
    for move in moves:
        copy(move, y).wait_send()
    for i in range(n_own // UNROLL):
        out_copy(i).wait()


def solution(mesh):
    n_y = mesh.shape["rows"]
    n_x = mesh.shape["ksplit"] // 2
    row_spec = P(("batch", "rows"), "ksplit")
    col_spec = P(("batch", "ksplit"))

    def device_step(a_loc, b_loc, pair_loc, plist_loc, cidx_loc):
        a, b = a_loc[0, 0], b_loc[0]
        n_a, size, _ = a.shape
        n_b = b.shape[0]
        n_own = cidx_loc.shape[2]
        n_part = plist_loc.shape[2]
        assert n_x == 4 and n_y == 4 and n_part == n_x * 128 and 128 % n_own == 0
        moves = plan(n_a, n_b, HALF_SET)
        any_space = pl.BlockSpec(memory_space=pl.ANY)
        out = pl.pallas_call(
            functools.partial(kernel, (n_x, n_y, n_a, n_b, n_own)),
            out_shape=jax.ShapeDtypeStruct((n_own, size, size), jnp.float32),
            in_specs=[any_space] * 5,
            out_specs=any_space,
            scratch_shapes=[pltpu.VMEM((n_a, size, size), jnp.bfloat16)] * 8
            + [pltpu.VMEM((n_b, size, size), jnp.bfloat16)] * 8
            + [
                pltpu.VMEM((n_own, size, size), jnp.float32),
                pltpu.VMEM((2, n_part), jnp.int32),
                pltpu.VMEM((2, n_part), jnp.int32),
                pltpu.VMEM((2, n_own), jnp.int32),
                pltpu.VMEM((8, 2, 128), jnp.int32),
                pltpu.VMEM((8, 2, 128), jnp.int32),
                pltpu.VMEM((2, 8, 128), jnp.int32),
                pltpu.SMEM((2, 8, 128), jnp.int32),
                pltpu.SemaphoreType.DMA((len(moves),)),
                pltpu.SemaphoreType.DMA((len(moves),)),
                pltpu.SemaphoreType.DMA((14,)),
                pltpu.SemaphoreType.DMA((14,)),
                pltpu.SemaphoreType.DMA((6,)),
                pltpu.SemaphoreType.DMA((n_own // UNROLL,)),
            ],
            compiler_params=pltpu.CompilerParams(
                collective_id=0, has_side_effects=True, vmem_limit_bytes=48 * 1024 * 1024
            ),
        )(a, b, pair_loc[0, 0, :, 0, :].T, plist_loc[0, 0].T, cidx_loc[0, 0].T)
        return out[None, None]

    return jax.shard_map(
        device_step, mesh=mesh, in_specs=(row_spec, col_spec, row_spec, row_spec, row_spec), out_specs=row_spec, check_vma=False
    )
```

time: 305 us -> 97.1 us (0.32)
  waiting for transfers between devices: 182 us -> 0 us
  Pallas kernels: 0 us -> 87.4 us
  local copies, waits for them, and re-layouts: 79.7 us -> 9.38 us
  matrix products: 29.3 us -> 0 us
  starting transfers between devices: 12.1 us -> 0 us
    all_to_all x2 -> x0, waiting for transfers between devices: 182 us -> none  [the longest x1 182 us: device_step(): recv_vals = lax.all_to_all(part_sums, 'ksplit', 0, 0, tiled=True)]
    pallas_call x0 -> x1, Pallas kernels: none -> 87.4 us  [device_step(): pl.pallas_call(functools.partial(kernel, (n_x, n_y, n_a, n_b, n_own)), ou...]
    dot_general x2 -> x0, matrix products: 29.3 us -> none  [the longest x1 18.8 us: device_step(): jnp.einsum('stab,stbc->sac', a_sel, b_sel, preferred_element_type=jnp.flo...]
    dot_general x2 -> x0, local copies, waits for them, and re-layouts: 29.2 us -> none  [device_step(): c_flat = jnp.dot(hit_mask, flat_vals, preferred_element_type=jnp.float32)]
    gather x2 -> x0, local copies, waits for them, and re-layouts: 28.7 us -> none  [the longest x1 14.8 us: device_step(): a_sel = jnp.take(a_blocks, pair_tab[:, :, 0], axis=0)]
    all_to_all x2 -> x0, starting transfers between devices: 12.1 us -> none  [the longest x1 6.08 us: device_step(): recv_vals = lax.all_to_all(part_sums, 'ksplit', 0, 0, tiled=True)]
    unnamed x9 -> x11, local copies, waits for them, and re-layouts: 20.2 us -> 9.38 us
  transfers between devices with their start and end apart: 2 -> 0, of which waited for: 1 -> 0; matrix products, arithmetic and copies ran while one was open for 16% -> 0% of each run, Pallas kernels for 0% -> 0%
where the time goes in v1:
time: 97.1 us; the launch traced here: 96.8 us
  Pallas kernels  87.4 us (90%)
  local copies, waits for them, and re-layouts  9.38 us (10%)
    pallas_call x1, Pallas kernels, device_step(): pl.pallas_call(functools.partial(kernel, (n_x, n_y, n_a, n_b, n_own)), ou...  87.4 us
    unnamed x11, local copies, waits for them, and re-layouts  9.38 us

profile of v1, /device:TPU:97, one launch (start us, length us, event | category | flops | bytes accessed | tf_op | source)
XLA Modules:
  0.0 96.8 jit_solution(12592731347899418231)
XLA Ops:
  0.0 0.0 copy-start
  0.0 1.6 %copy-done = bf16[1,64,128,128]{3,2,1,0:T(8,128)(2,1)S(1)} copy-done((bf16[1,64,128,128]{3,2,1,0:T(8,128)(2,1)S(1)}, bf16[1,64,128,128]{3,2,1,0:T(8,128)(2,1)}, u32[]{:S(2)}) %copy-start) | copy-done | bytes 2097176
  1.6 0.0 copy-start.1
  1.6 1.0 %copy-done.1 = bf16[1,1,16,128,128]{4,3,2,1,0:T(8,128)(2,1)S(1)} copy-done((bf16[1,1,16,128,128]{4,3,2,1,0:T(8,128)(2,1)S(1)}, bf16[1,1,16,128,128]{4,3,2,1,0:T(8,128)(2,1)}, u32[]{:S(2)}) %copy-start.1) | copy-done | bytes 524312
  2.6 0.0 copy-start.2
  2.6 0.7 copy-done.2
  3.3 0.0 copy-start.3
  3.3 0.7 copy-done.3
  4.0 0.0 copy-start.4
  4.0 0.7 copy-done.4
  4.7 87.4 %shard_map.55 = f32[64,128,128]{2,1,0:T(8,128)} custom-call(bf16[16,128,128]{2,1,0:T(8,128)(2,1)S(1)} %bitcast.13, bf16[64,128,128]{2,1,0:T(8,128)(2,1)S(1)} %bitcast.12, s32[2,512]{1,0:T(2,128)S(1)} %bitcast.14, s32[2,512]{1,0:T(2,128)S(1)} %bitcast.15, s32[2,64]{1,0:T(2,128)S(1)} %bitcast.16), custom_call_target="tpu_custom_call" | custom-call | tf_op jit(solution)/shard_map/pallas_call | solution.py:329
  92.1 4.7 %copy.7 = f32[1,1,64,128,128]{4,3,2,1,0:T(8,128)} copy(f32[1,1,64,128,128]{4,3,2,1,0:T(8,128)} %bitcast.17) | data formatting | bytes 8388608
Async XLA Ops:
  0.0 1.6 %copy-start = (bf16[1,64,128,128]{3,2,1,0:T(8,128)(2,1)S(1)}, bf16[1,64,128,128]{3,2,1,0:T(8,128)(2,1)}, u32[]{:S(2)}) copy-start(bf16[1,64,128,128]{3,2,1,0:T(8,128)(2,1)} %param.6) | copy-start | bytes 6291460
  1.6 1.0 %copy-start.1 = (bf16[1,1,16,128,128]{4,3,2,1,0:T(8,128)(2,1)S(1)}, bf16[1,1,16,128,128]{4,3,2,1,0:T(8,128)(2,1)}, u32[]{:S(2)}) copy-start(bf16[1,1,16,128,128]{4,3,2,1,0:T(8,128)(2,1)} %param.5) | copy-start | bytes 1572868
  2.6 0.7 copy-start.2
  3.3 0.7 copy-start.3
  4.0 0.7 copy-start.4

commit v2 on v1

--- a/solution.py
+++ b/solution.py
@@ -10,97 +10,113 @@
 MESH = pl.DeviceIdType.MESH
 HALF_SET = 32
 CHUNK = 4
+A_CHUNK = 4
+WINDOW = 2
+TABLE_AT = 9.0
+LAG = 3.0
 UNROLL = 8
-FRONT = 8
 
 
 class Move:
-    def __init__(self, link, kind, src, dst, part, first, count, dep):
+    def __init__(self, link, kind, src, dst, part, first, count, dep, shift, rank):
         self.link, self.kind, self.src, self.dst = link, kind, src, dst
         self.part, self.first, self.count, self.dep = part, first, count, dep
+        self.shift = shift
+        self.rank = rank
         self.after = []
-        self.shift = 0
-        self.arrive = None
 
 
 def cut(first, count, size):
     return [(first + at, min(size, count - at)) for at in range(0, count, size)]
 
 
-def plan(n_a, n_b, half_set):
-    half = half_set // 2
-    quarter = (n_b - half_set) // 4
+def plan(n_a, n_b):
+    half = HALF_SET // 2
+    quarter = (n_b - HALF_SET) // 4
     h1, h2 = cut(0, half // 2, CHUNK), cut(half // 2, half - half // 2, CHUNK)
     q1, q2 = cut(0, quarter // 2, CHUNK), cut(quarter // 2, quarter - quarter // 2, CHUNK)
-    a1, a2 = (0, n_a // 2), (n_a // 2, n_a - n_a // 2)
+    a1, a2 = cut(0, n_a // 2, A_CHUNK), cut(n_a // 2, n_a - n_a // 2, A_CHUNK)
     moves = []
 
-    def add(link, kind, src, dst, part, piece, dep, shift=0):
-        move = Move(link, kind, src, dst, part, piece[0], piece[1], dep)
-        move.shift = shift
+    def add(link, kind, src, dst, part, piece, dep, rank, shift=0):
+        move = Move(link, kind, src, dst, part, piece[0], piece[1], dep, shift, rank)
         move.index = len(moves)
         moves.append(move)
         if dep is not None:
             dep.after.append(move)
         if link != "d":
-            add_pair(move)
+            row = {"+y": -1, "-y": 1}.get(link, 0) + shift
+            add("d", kind, dst, dst, part, piece, move, 0, row)
         return move
 
-    def add_pair(move):
-        row = {"+y": -1, "-y": 1}.get(move.link, 0) + move.shift
-        add("d", move.kind, move.dst, move.dst, move.part, (move.first, move.count), move, row)
-
-    def spread(move, up, down, piece):
-        for link in ("+y",) * up + ("-y",) * down:
-            step = 1 if link == "+y" else -1
-            nxt = add(link, "b", move.dst, move.dst, move.part, piece, move)
-            if move.part == "q":
-                if (link == "+y" and piece in q1) or (link == "-y" and piece in q2):
-                    add(link, "b", move.dst, move.dst, "q", piece, nxt, -step)
-
-    def over_x(link, back, pieces, part, group):
-        out = []
-        for piece in pieces:
-            move = add(link, "b", 0, back, part, piece, None)
-            out.append((move, piece, group))
-        return out
-
-    add("d", "b", 0, 0, "all", (0, n_b), None)
-    add("d", "a", 0, 0, "all", (0, n_a), None)
-    right = over_x("+x", 3, h1, "h", 1) + over_x("+x", 3, h2, "h", 2) + over_x("+x", 3, q1, "q", 1) + over_x("+x", 3, q2, "q", 2)
-    left = over_x("-x", 1, h2, "h", 2) + over_x("-x", 1, h1, "h", 1) + over_x("-x", 1, q2, "q", 2) + over_x("-x", 1, q1, "q", 1)
-    for received, link, keep in ((right, "+x", 1), (left, "-x", 2)):
-        for move, piece, group in received:
-            spread(move, move.part == "q" or group == 1, move.part == "q" or group == 2, piece)
-            if group == keep:
-                nxt = add(link, "b", move.dst, 2, move.part, piece, move)
-                spread(nxt, nxt.part == "q" or group == 1, nxt.part == "q" or group == 2, piece)
-    late = []
-    for (received, link, back, half_a) in ((right, "+x", 3, a1), (left, "-x", 1, a2)):
-        for piece in (a1, a2) if link == "+x" else (a2, a1):
-            move = add(link, "a", 0, back, "all", piece, received[-1][0])
-            if piece == half_a:
-                add(link, "a", move.dst, 2, "all", piece, move)
+    def spread(move, piece, far):
+        if move.part == "h":
+            add("+y" if piece in h1 else "-y", "b", move.dst, move.dst, "h", piece, move, far + 1)
+            return
+        up = add("+y", "b", move.dst, move.dst, "q", piece, move, far)
+        down = add("-y", "b", move.dst, move.dst, "q", piece, move, far)
+        if piece in q1:
+            add("+y", "b", move.dst, move.dst, "q", piece, up, far + 2, -1)
+        else:
+            add("-y", "b", move.dst, move.dst, "q", piece, down, far + 2, 1)
+
+    for kind, count in (("b", n_b), ("a", n_a)):
+        add("d", kind, 0, 0, "all", (0, count), None, 9)
+    for link, slot in (("+x", 3), ("-x", 1)):
+        first = link == "+x"
+        for part, one, two in (("q", q1, q2), ("h", h1, h2)):
+            keep = one if first else two
+            for piece in (one + two) if first else (two + one):
+                move = add(link, "b", 0, slot, part, piece, None, 0)
+                spread(move, piece, 0)
+                if piece in keep:
+                    spread(add(link, "b", slot, 2, part, piece, move, 1), piece, 3)
+        keep = a1 if first else a2
+        for piece in (a1 + a2) if first else (a2 + a1):
+            move = add(link, "a", 0, slot, "all", piece, None, 2)
+            if piece in keep:
+                add(link, "a", slot, 2, "all", piece, move, 3)
     return moves
 
 
-def expected(moves):
-    free = {"+x": 0.0, "-x": 0.0, "+y": 0.0, "-y": 0.0, "d": 0.0}
-    lag = {"+x": 2.6, "-x": 2.6, "+y": 2.6, "-y": 2.6, "d": 1.4}
-    ready = [(0.0, i, m) for i, m in enumerate(moves) if m.dep is None]
-    order = []
-    count = len(moves)
-    while ready:
-        ready.sort(key=lambda item: (item[0], item[1]))
-        at, _, move = ready.pop(0)
-        begin = max(at, free[move.link])
-        free[move.link] = begin + move.count * (0.1 if move.link == "d" else 1.0)
-        move.arrive = free[move.link] + lag[move.link]
-        order.append(move)
+LINKS = ("+x", "-x", "+y", "-y")
+
+
+def order(moves):
+    waiting = {link: [m for m in moves if m.link == link and m.dep is None] for link in LINKS}
+    flying = {link: 0 for link in LINKS}
+    free = {link: 0.0 for link in LINKS}
+    events, steps, now = [], [], 0.0
+
+    def send():
+        for link in LINKS:
+            waiting[link].sort(key=lambda m: (m.rank, m.index))
+        busy = True
+        while busy:
+            busy = False
+            for link in LINKS:
+                if waiting[link] and flying[link] < WINDOW:
+                    move = waiting[link].pop(0)
+                    flying[link] += 1
+                    free[link] = max(now, free[link]) + move.count
+                    events.append((free[link] + LAG, move.index, move))
+                    steps.append((now, "send", move))
+                    busy = True
+
+    send()
+    while events:
+        events.sort(key=lambda e: e[:2])
+        now, _, move = events.pop(0)
+        flying[move.link] -= 1
+        steps.append((now, "take", move))
         for nxt in move.after:
-            ready.append((move.arrive, nxt.index, nxt))
-    assert len(order) == count
-    return sorted(moves, key=lambda m: (m.arrive, m.index))
+            if nxt.link == "d":
+                steps.append((now, "send", nxt))
+            else:
+                waiting[nxt.link].append(nxt)
+        send()
+    assert not any(waiting.values())
+    return steps
 
 
 def kernel(sizes, a_hbm, b_hbm, pairs_hbm, plist_hbm, own_hbm, out_hbm, *scratch):
@@ -111,8 +127,8 @@
     y = lax.axis_index("rows")
     p = lax.axis_index("ksplit")
     x, core = p // 2, p % 2
-    moves = plan(n_a, n_b, HALF_SET)
-    arrivals = expected(moves)
+    moves = plan(n_a, n_b)
+    steps = order(moves)
 
     def at(dx, other):
         return 2 * ((x + dx) % n_x) + (core + other) % 2
@@ -198,17 +214,22 @@
             ))
         return pair
 
-    loads[0].wait()
-    for move in moves:
-        if move.dep is None and move.kind == "b" and move.link != "d":
+    def run(step):
+        _, what, move = step
+        if what == "send":
             start(move)
-    for load in loads[1:]:
+        else:
+            receive(move)
+
+    for load in loads:
         load.wait()
+    while steps[0][1] == "send":
+        run(steps.pop(0))
     for number, (dx, other) in enumerate(peers):
         for one in lists(number, dx, other):
             one.start()
     for move in moves:
-        if move.dep is None and (move.kind == "a" or move.link == "d"):
+        if move.dep is None and move.link == "d":
             start(move)
 
     def make_table():
@@ -244,7 +265,7 @@
         part = jnp.dot(left, right, preferred_element_type=jnp.float32)
         return part.astype(jnp.bfloat16).astype(jnp.float32)
 
-    def compute(slots, first=False, last=False):
+    def compute(slots, part=(0, 1), first=False, last=False):
         def step(i, _):
             for u in range(UNROLL):
                 c = i * UNROLL + u
@@ -256,51 +277,50 @@
                 out_copy(i).start()
             return 0
 
-        lax.fori_loop(0, n_own // UNROLL, step, 0)
+        count = n_own // UNROLL // part[1]
+        lax.fori_loop(part[0] * count, (part[0] + 1) * count, step, 0)
 
     def out_copy(i):
         where = pl.ds(i * UNROLL, UNROLL)
         return pltpu.make_async_copy(acc.at[where], out_hbm.at[where], out_sem.at[i])
 
-    seen = set()
-
-    def take(move):
-        if move.index not in seen:
-            seen.add(move.index)
-            receive(move)
-            for nxt in move.after:
-                start(nxt)
-
-    def need(dx, other):
-        return [m for m in arrivals if m.dst == dx and (m.link == "d") == bool(other)]
-
-    wire = [m for m in arrivals if m.link != "d"]
-    early = [m for m in wire if m.arrive < 10.0]
-    for move in early:
-        take(move)
-    make_table()
-    for move in wire:
-        if move.arrive < 14.0:
-            take(move)
-    use_table()
-    for move in need(0, 1):
-        take(move)
-    compute((0, 1), first=True)
-    done = {0}
-    for position, move in enumerate(wire):
-        take(move)
-        rest = [m for m in wire[position + 1:]]
-        for dx in (3, 1):
-            if dx not in done and not [m for m in rest if m.dst == dx]:
-                done.add(dx)
-                for m in need(dx, 1):
-                    take(m)
-                compute((2 * dx, 2 * dx + 1))
+    def from_partner(dx):
+        for move in moves:
+            if move.link == "d" and move.dst == dx:
+                receive(move)
+
+    jobs = []
+    queued = set()
+    stage = 0
+
+    def ready(dx):
+        return not [s for s in steps if s[1] == "take" and s[2].dst == dx]
+
+    while steps:
+        now = steps[0][0]
+        if stage == 0 and now > TABLE_AT:
+            make_table()
+            stage = 1
+        elif stage == 1 and now > TABLE_AT + 3.0:
+            use_table()
+            from_partner(0)
+            jobs += [functools.partial(compute, (0, 1), (i, 2), first=True) for i in range(2)]
+            stage = 2
+        run(steps.pop(0))
+        while steps and steps[0][1] == "send":
+            run(steps.pop(0))
+        for dx in (1, 3):
+            if dx not in queued and ready(dx):
+                queued.add(dx)
+                jobs.append(functools.partial(from_partner, dx))
+                jobs += [functools.partial(compute, (2 * dx, 2 * dx + 1), (i, 2)) for i in range(2)]
+        if jobs:
+            jobs.pop(0)()
+    for job in jobs:
+        job()
     compute((4,))
-    for m in need(2, 1):
-        take(m)
+    from_partner(2)
     compute((5,), last=True)
-    assert len(seen) == len(moves)
 
     for number, (dx, other) in enumerate(peers):
         for one in lists(number, dx, other):
@@ -324,13 +344,13 @@
         n_own = cidx_loc.shape[2]
         n_part = plist_loc.shape[2]
         assert n_x == 4 and n_y == 4 and n_part == n_x * 128 and 128 % n_own == 0
-        moves = plan(n_a, n_b, HALF_SET)
-        any_space = pl.BlockSpec(memory_space=pl.ANY)
+        moves = plan(n_a, n_b)
+        in_hbm = pl.BlockSpec(memory_space=pltpu.HBM)
         out = pl.pallas_call(
             functools.partial(kernel, (n_x, n_y, n_a, n_b, n_own)),
             out_shape=jax.ShapeDtypeStruct((n_own, size, size), jnp.float32),
-            in_specs=[any_space] * 5,
-            out_specs=any_space,
+            in_specs=[in_hbm] * 5,
+            out_specs=in_hbm,
             scratch_shapes=[pltpu.VMEM((n_a, size, size), jnp.bfloat16)] * 8
             + [pltpu.VMEM((n_b, size, size), jnp.bfloat16)] * 8
             + [

time: 97.1 us -> 84.6 us (0.87)
  Pallas kernels: 87.4 us -> 74.9 us
    pallas_call x1, Pallas kernels: 87.4 us -> 74.9 us  [device_step(): pl.pallas_call(functools.partial(kernel, (n_x, n_y, n_a, n_b, n_own)), ou...]
where the time goes in v2:
time: 84.6 us; the launch traced here: 84.3 us
  Pallas kernels  74.9 us (89%)
  local copies, waits for them, and re-layouts  9.38 us (11%)
    pallas_call x1, Pallas kernels, device_step(): pl.pallas_call(functools.partial(kernel, (n_x, n_y, n_a, n_b, n_own)), ou...  74.9 us
    unnamed x11, local copies, waits for them, and re-layouts  9.38 us

profile of v2, /device:TPU:97, one launch (start us, length us, event | category | flops | bytes accessed | tf_op | source)
XLA Modules:
  0.0 84.3 jit_solution(16461701719128140427)
XLA Ops:
  0.0 0.0 copy-start
  0.0 1.6 %copy-done = bf16[1,64,128,128]{3,2,1,0:T(8,128)(2,1)S(1)} copy-done((bf16[1,64,128,128]{3,2,1,0:T(8,128)(2,1)S(1)}, bf16[1,64,128,128]{3,2,1,0:T(8,128)(2,1)}, u32[]{:S(2)}) %copy-start) | copy-done | bytes 2097176
  1.6 0.0 copy-start.1
  1.6 1.0 %copy-done.1 = bf16[1,1,16,128,128]{4,3,2,1,0:T(8,128)(2,1)S(1)} copy-done((bf16[1,1,16,128,128]{4,3,2,1,0:T(8,128)(2,1)S(1)}, bf16[1,1,16,128,128]{4,3,2,1,0:T(8,128)(2,1)}, u32[]{:S(2)}) %copy-start.1) | copy-done | bytes 524312
  2.6 0.0 copy-start.2
  2.6 0.7 copy-done.2
  3.3 0.0 copy-start.3
  3.3 0.7 copy-done.3
  4.0 0.0 copy-start.4
  4.0 0.7 copy-done.4
  4.7 74.9 %shard_map.55 = f32[64,128,128]{2,1,0:T(8,128)} custom-call(bf16[16,128,128]{2,1,0:T(8,128)(2,1)S(1)} %bitcast.13, bf16[64,128,128]{2,1,0:T(8,128)(2,1)S(1)} %bitcast.12, s32[2,512]{1,0:T(2,128)S(1)} %bitcast.14, s32[2,512]{1,0:T(2,128)S(1)} %bitcast.15, s32[2,64]{1,0:T(2,128)S(1)} %bitcast.16), custom_call_target="tpu_custom_call" | custom-call | tf_op jit(solution)/shard_map/pallas_call | solution.py:349
  79.6 4.7 %copy.7 = f32[1,1,64,128,128]{4,3,2,1,0:T(8,128)} copy(f32[1,1,64,128,128]{4,3,2,1,0:T(8,128)} %bitcast.17) | data formatting | bytes 8388608
Async XLA Ops:
  0.0 1.6 %copy-start = (bf16[1,64,128,128]{3,2,1,0:T(8,128)(2,1)S(1)}, bf16[1,64,128,128]{3,2,1,0:T(8,128)(2,1)}, u32[]{:S(2)}) copy-start(bf16[1,64,128,128]{3,2,1,0:T(8,128)(2,1)} %param.6) | copy-start | bytes 6291460
  1.6 1.0 %copy-start.1 = (bf16[1,1,16,128,128]{4,3,2,1,0:T(8,128)(2,1)S(1)}, bf16[1,1,16,128,128]{4,3,2,1,0:T(8,128)(2,1)}, u32[]{:S(2)}) copy-start(bf16[1,1,16,128,128]{4,3,2,1,0:T(8,128)(2,1)} %param.5) | copy-start | bytes 1572868
  2.6 0.7 copy-start.2
  3.3 0.7 copy-start.3
  4.0 0.7 copy-start.4

commit v3 on v2

--- a/solution.py
+++ b/solution.py
@@ -11,8 +11,9 @@
 HALF_SET = 32
 CHUNK = 4
 A_CHUNK = 4
-WINDOW = 2
+WINDOW = 3
 TABLE_AT = 9.0
+VMEM = 67_000_000
 LAG = 3.0
 UNROLL = 8
 
@@ -370,7 +371,7 @@
                 pltpu.SemaphoreType.DMA((n_own // UNROLL,)),
             ],
             compiler_params=pltpu.CompilerParams(
-                collective_id=0, has_side_effects=True, vmem_limit_bytes=48 * 1024 * 1024
+                collective_id=0, has_side_effects=True, vmem_limit_bytes=VMEM
             ),
         )(a, b, pair_loc[0, 0, :, 0, :].T, plist_loc[0, 0].T, cidx_loc[0, 0].T)
         return out[None, None]

time: 84.6 us -> 78.4 us (0.927)
  local copies, waits for them, and re-layouts: 9.38 us -> 4.7 us
  Pallas kernels: 74.9 us -> 73.6 us
    unnamed x11 -> x1, local copies, waits for them, and re-layouts: 9.38 us -> 4.7 us
    pallas_call x1, Pallas kernels: 74.9 us -> 73.6 us  [device_step(): pl.pallas_call(functools.partial(kernel, (n_x, n_y, n_a, n_b, n_own)), ou...]
where the time goes in v3:
time: 78.4 us; the launch traced here: 78.3 us
  Pallas kernels  73.6 us (94%)
  local copies, waits for them, and re-layouts  4.7 us (6%)
    pallas_call x1, Pallas kernels, device_step(): pl.pallas_call(functools.partial(kernel, (n_x, n_y, n_a, n_b, n_own)), ou...  73.6 us
    unnamed x1, local copies, waits for them, and re-layouts  4.7 us

profile of v3, /device:TPU:97, one launch (start us, length us, event | category | flops | bytes accessed | tf_op | source)
XLA Modules:
  0.0 78.3 jit_solution(1354663713197940905)
XLA Ops:
  0.0 73.6 %shard_map.55 = f32[64,128,128]{2,1,0:T(8,128)} custom-call(bf16[16,128,128]{2,1,0:T(8,128)(2,1)} %bitcast.14, bf16[64,128,128]{2,1,0:T(8,128)(2,1)} %bitcast.13, s32[2,512]{1,0:T(2,128)} %bitcast.15, s32[2,512]{1,0:T(2,128)} %bitcast.16, s32[2,64]{1,0:T(2,128)} %bitcast.17), custom_call_target="tpu_custom_call" | custom-call | tf_op jit(solution)/shard_map/pallas_call | solution.py:350
  73.6 4.7 %copy.7 = f32[1,1,64,128,128]{4,3,2,1,0:T(8,128)} copy(f32[1,1,64,128,128]{4,3,2,1,0:T(8,128)} %bitcast.12) | data formatting | bytes 8388608

commit v4 on v3

--- a/solution.py
+++ b/solution.py
@@ -11,7 +11,8 @@
 HALF_SET = 32
 CHUNK = 4
 A_CHUNK = 4
-WINDOW = 3
+WINDOW = 1
+GAP = 0.2
 TABLE_AT = 9.0
 VMEM = 67_000_000
 LAG = 3.0
@@ -85,7 +86,7 @@
 
 def order(moves):
     waiting = {link: [m for m in moves if m.link == link and m.dep is None] for link in LINKS}
-    flying = {link: 0 for link in LINKS}
+    flying = {link: [] for link in LINKS}
     free = {link: 0.0 for link in LINKS}
     events, steps, now = [], [], 0.0
 
@@ -96,25 +97,29 @@
         while busy:
             busy = False
             for link in LINKS:
-                if waiting[link] and flying[link] < WINDOW:
+                if waiting[link] and len([m for m in flying[link] if m.leaves > now]) < WINDOW:
                     move = waiting[link].pop(0)
-                    flying[link] += 1
+                    if len(flying[link]) == WINDOW:
+                        steps.append((now, "sent", flying[link].pop(0)))
+                    flying[link].append(move)
                     free[link] = max(now, free[link]) + move.count
-                    events.append((free[link] + LAG, move.index, move))
+                    move.leaves = free[link] + GAP
+                    events.append((move.leaves, 0, move.index, move))
+                    events.append((free[link] + LAG, 1, move.index, move))
                     steps.append((now, "send", move))
                     busy = True
 
     send()
     while events:
-        events.sort(key=lambda e: e[:2])
-        now, _, move = events.pop(0)
-        flying[move.link] -= 1
-        steps.append((now, "take", move))
-        for nxt in move.after:
-            if nxt.link == "d":
-                steps.append((now, "send", nxt))
-            else:
-                waiting[nxt.link].append(nxt)
+        events.sort(key=lambda e: e[:3])
+        now, come, _, move = events.pop(0)
+        if come:
+            steps.append((now, "take", move))
+            for nxt in move.after:
+                if nxt.link == "d":
+                    steps.append((now, "send", nxt))
+                else:
+                    waiting[nxt.link].append(nxt)
         send()
     assert not any(waiting.values())
     return steps
@@ -215,10 +220,15 @@
             ))
         return pair
 
+    sent = set()
+
     def run(step):
         _, what, move = step
         if what == "send":
             start(move)
+        elif what == "sent":
+            copy(move, y).wait_send()
+            sent.add(move.index)
         else:
             receive(move)
 
@@ -308,7 +318,7 @@
             jobs += [functools.partial(compute, (0, 1), (i, 2), first=True) for i in range(2)]
             stage = 2
         run(steps.pop(0))
-        while steps and steps[0][1] == "send":
+        while steps and steps[0][1] != "take":
             run(steps.pop(0))
         for dx in (1, 3):
             if dx not in queued and ready(dx):
@@ -327,7 +337,8 @@
         for one in lists(number, dx, other):
             one.wait_send()
     for move in moves:
-        copy(move, y).wait_send()
+        if move.index not in sent:
+            copy(move, y).wait_send()
     for i in range(n_own // UNROLL):
         out_copy(i).wait()
 

time: 78.4 us -> 84.9 us (1.083)
  Pallas kernels: 73.6 us -> 80.1 us
    pallas_call x1, Pallas kernels: 73.6 us -> 80.1 us  [device_step(): pl.pallas_call(functools.partial(kernel, (n_x, n_y, n_a, n_b, n_own)), ou...]
where the time goes in v4:
time: 84.9 us; the launch traced here: 84.8 us
  Pallas kernels  80.1 us (94%)
  local copies, waits for them, and re-layouts  4.7 us (6%)
    pallas_call x1, Pallas kernels, device_step(): pl.pallas_call(functools.partial(kernel, (n_x, n_y, n_a, n_b, n_own)), ou...  80.1 us
    unnamed x1, local copies, waits for them, and re-layouts  4.7 us

profile of v4, /device:TPU:97, one launch (start us, length us, event | category | flops | bytes accessed | tf_op | source)
XLA Modules:
  0.0 84.8 jit_solution(956170821934926640)
XLA Ops:
  0.0 80.1 %shard_map.55 = f32[64,128,128]{2,1,0:T(8,128)} custom-call(bf16[16,128,128]{2,1,0:T(8,128)(2,1)} %bitcast.14, bf16[64,128,128]{2,1,0:T(8,128)(2,1)} %bitcast.13, s32[2,512]{1,0:T(2,128)} %bitcast.15, s32[2,512]{1,0:T(2,128)} %bitcast.16, s32[2,64]{1,0:T(2,128)} %bitcast.17), custom_call_target="tpu_custom_call" | custom-call | tf_op jit(solution)/shard_map/pallas_call | solution.py:361
  80.1 4.7 %copy.7 = f32[1,1,64,128,128]{4,3,2,1,0:T(8,128)} copy(f32[1,1,64,128,128]{4,3,2,1,0:T(8,128)} %bitcast.12) | data formatting | bytes 8388608

commit v5 on v3

--- a/solution.py
+++ b/solution.py
@@ -8,7 +8,7 @@
 from jax.sharding import PartitionSpec as P
 
 MESH = pl.DeviceIdType.MESH
-HALF_SET = 32
+HALF_SET = 64
 CHUNK = 4
 A_CHUNK = 4
 WINDOW = 3

time: 78.4 us -> 83.2 us (1.061)
  Pallas kernels: 73.6 us -> 78.3 us
    pallas_call x1, Pallas kernels: 73.6 us -> 78.3 us  [device_step(): pl.pallas_call(functools.partial(kernel, (n_x, n_y, n_a, n_b, n_own)), ou...]
where the time goes in v5:
time: 83.2 us; the launch traced here: 83 us
  Pallas kernels  78.3 us (94%)
  local copies, waits for them, and re-layouts  4.7 us (6%)
    pallas_call x1, Pallas kernels, device_step(): pl.pallas_call(functools.partial(kernel, (n_x, n_y, n_a, n_b, n_own)), ou...  78.3 us
    unnamed x1, local copies, waits for them, and re-layouts  4.7 us

profile of v5, /device:TPU:97, one launch (start us, length us, event | category | flops | bytes accessed | tf_op | source)
XLA Modules:
  0.0 83.0 jit_solution(4705769548324960893)
XLA Ops:
  0.0 78.3 %shard_map.55 = f32[64,128,128]{2,1,0:T(8,128)} custom-call(bf16[16,128,128]{2,1,0:T(8,128)(2,1)} %bitcast.14, bf16[64,128,128]{2,1,0:T(8,128)(2,1)} %bitcast.13, s32[2,512]{1,0:T(2,128)} %bitcast.15, s32[2,512]{1,0:T(2,128)} %bitcast.16, s32[2,64]{1,0:T(2,128)} %bitcast.17), custom_call_target="tpu_custom_call" | custom-call | tf_op jit(solution)/shard_map/pallas_call | solution.py:350
  78.3 4.7 %copy.7 = f32[1,1,64,128,128]{4,3,2,1,0:T(8,128)} copy(f32[1,1,64,128,128]{4,3,2,1,0:T(8,128)} %bitcast.12) | data formatting | bytes 8388608

commit v6 on v3

--- a/solution.py
+++ b/solution.py
@@ -9,9 +9,9 @@
 
 MESH = pl.DeviceIdType.MESH
 HALF_SET = 32
-CHUNK = 4
-A_CHUNK = 4
-WINDOW = 3
+CHUNK = 8
+A_CHUNK = 8
+WINDOW = 2
 TABLE_AT = 9.0
 VMEM = 67_000_000
 LAG = 3.0

time: 78.4 us -> 76.5 us (0.976)
  Pallas kernels: 73.6 us -> 71.6 us
    pallas_call x1, Pallas kernels: 73.6 us -> 71.6 us  [device_step(): pl.pallas_call(functools.partial(kernel, (n_x, n_y, n_a, n_b, n_own)), ou...]
where the time goes in v6:
time: 76.5 us; the launch traced here: 76.3 us
  Pallas kernels  71.6 us (94%)
  local copies, waits for them, and re-layouts  4.7 us (6%)
    pallas_call x1, Pallas kernels, device_step(): pl.pallas_call(functools.partial(kernel, (n_x, n_y, n_a, n_b, n_own)), ou...  71.6 us
    unnamed x1, local copies, waits for them, and re-layouts  4.7 us

profile of v6, /device:TPU:97, one launch (start us, length us, event | category | flops | bytes accessed | tf_op | source)
XLA Modules:
  0.0 76.3 jit_solution(3738160835573913405)
XLA Ops:
  0.0 71.6 %shard_map.55 = f32[64,128,128]{2,1,0:T(8,128)} custom-call(bf16[16,128,128]{2,1,0:T(8,128)(2,1)} %bitcast.14, bf16[64,128,128]{2,1,0:T(8,128)(2,1)} %bitcast.13, s32[2,512]{1,0:T(2,128)} %bitcast.15, s32[2,512]{1,0:T(2,128)} %bitcast.16, s32[2,64]{1,0:T(2,128)} %bitcast.17), custom_call_target="tpu_custom_call" | custom-call | tf_op jit(solution)/shard_map/pallas_call | solution.py:350
  71.6 4.7 %copy.7 = f32[1,1,64,128,128]{4,3,2,1,0:T(8,128)} copy(f32[1,1,64,128,128]{4,3,2,1,0:T(8,128)} %bitcast.12) | data formatting | bytes 8388608

commit v7 on v5

--- a/solution.py
+++ b/solution.py
@@ -8,13 +8,14 @@
 from jax.sharding import PartitionSpec as P
 
 MESH = pl.DeviceIdType.MESH
-HALF_SET = 64
-CHUNK = 4
+HALF_SET = 40
+CHUNK = 5
 A_CHUNK = 4
-WINDOW = 3
-TABLE_AT = 9.0
+WINDOW = 6
+TABLE_AT = 6.0
 VMEM = 67_000_000
 LAG = 3.0
+PIECES = 4
 UNROLL = 8
 
 
@@ -222,13 +223,15 @@
         else:
             receive(move)
 
-    for load in loads:
+    for load in loads[2:]:
+        load.wait()
+    for number, (dx, other) in enumerate(peers):
+        for one in lists(number, dx, other):
+            one.start()
+    for load in loads[:2]:
         load.wait()
     while steps[0][1] == "send":
         run(steps.pop(0))
-    for number, (dx, other) in enumerate(peers):
-        for one in lists(number, dx, other):
-            one.start()
     for move in moves:
         if move.dep is None and move.link == "d":
             start(move)
@@ -305,7 +308,7 @@
         elif stage == 1 and now > TABLE_AT + 3.0:
             use_table()
             from_partner(0)
-            jobs += [functools.partial(compute, (0, 1), (i, 2), first=True) for i in range(2)]
+            jobs += [functools.partial(compute, (0, 1), (i, PIECES), first=True) for i in range(PIECES)]
             stage = 2
         run(steps.pop(0))
         while steps and steps[0][1] == "send":
@@ -314,7 +317,7 @@
             if dx not in queued and ready(dx):
                 queued.add(dx)
                 jobs.append(functools.partial(from_partner, dx))
-                jobs += [functools.partial(compute, (2 * dx, 2 * dx + 1), (i, 2)) for i in range(2)]
+                jobs += [functools.partial(compute, (2 * dx, 2 * dx + 1), (i, PIECES)) for i in range(PIECES)]
         if jobs:
             jobs.pop(0)()
     for job in jobs:

time: 83.2 us -> 73.1 us (0.88)
  Pallas kernels: 78.3 us -> 68.2 us
    pallas_call x1, Pallas kernels: 78.3 us -> 68.2 us  [device_step(): pl.pallas_call(functools.partial(kernel, (n_x, n_y, n_a, n_b, n_own)), ou...]
where the time goes in v7:
time: 73.1 us; the launch traced here: 72.9 us
  Pallas kernels  68.2 us (93%)
  local copies, waits for them, and re-layouts  4.7 us (6%)
    pallas_call x1, Pallas kernels, device_step(): pl.pallas_call(functools.partial(kernel, (n_x, n_y, n_a, n_b, n_own)), ou...  68.2 us
    unnamed x1, local copies, waits for them, and re-layouts  4.7 us

profile of v7, /device:TPU:97, one launch (start us, length us, event | category | flops | bytes accessed | tf_op | source)
XLA Modules:
  0.0 72.9 jit_solution(7959760877159720899)
XLA Ops:
  0.0 68.2 %shard_map.55 = f32[64,128,128]{2,1,0:T(8,128)} custom-call(bf16[16,128,128]{2,1,0:T(8,128)(2,1)} %bitcast.14, bf16[64,128,128]{2,1,0:T(8,128)(2,1)} %bitcast.13, s32[2,512]{1,0:T(2,128)} %bitcast.15, s32[2,512]{1,0:T(2,128)} %bitcast.16, s32[2,64]{1,0:T(2,128)} %bitcast.17), custom_call_target="tpu_custom_call" | custom-call | tf_op jit(solution)/shard_map/pallas_call | solution.py:353
  68.2 4.7 %copy.7 = f32[1,1,64,128,128]{4,3,2,1,0:T(8,128)} copy(f32[1,1,64,128,128]{4,3,2,1,0:T(8,128)} %bitcast.12) | data formatting | bytes 8388608

commit v8 on v7

--- a/solution.py
+++ b/solution.py
@@ -15,6 +15,8 @@
 TABLE_AT = 6.0
 VMEM = 67_000_000
 LAG = 3.0
+LATE = (4, 5)
+JOB = 0.8
 PIECES = 4
 UNROLL = 8
 
@@ -121,11 +123,13 @@
     return steps
 
 
-def kernel(sizes, a_hbm, b_hbm, pairs_hbm, plist_hbm, own_hbm, out_hbm, *scratch):
+def gather_kernel(sizes, a_hbm, b_hbm, pairs_hbm, plist_hbm, own_hbm, acc, table_v, *refs):
     n_x, n_y, n_a, n_b, n_own = sizes
-    a_slot, b_slot = scratch[0:8], scratch[8:16]
-    (acc, pairs_own, plist_own, own, pairs_in, plist_in, table_v, table,
-     send_sem, recv_sem, list_send, list_recv, load_sem, out_sem) = scratch[16:]
+    a_slot, b_slot = list(refs[0:8]), list(refs[8:16])
+    for place, slot in enumerate(LATE + tuple(s for s in range(8) if s not in LATE)):
+        a_slot[slot], b_slot[slot] = refs[2 * place], refs[2 * place + 1]
+    (pairs_own, plist_own, own, pairs_in, plist_in, table,
+     send_sem, recv_sem, list_send, list_recv, load_sem) = refs[16:]
     y = lax.axis_index("rows")
     p = lax.axis_index("ksplit")
     x, core = p // 2, p % 2
@@ -263,43 +267,30 @@
         to_smem.start()
         to_smem.wait()
 
-    def product(slot, c):
-        left = a_slot[slot][table[0, slot, c]]
-        right = b_slot[slot][table[1, slot, c]]
-        part = jnp.dot(left, right, preferred_element_type=jnp.float32)
-        return part.astype(jnp.bfloat16).astype(jnp.float32)
-
-    def compute(slots, part=(0, 1), first=False, last=False):
+    def compute(slots, part, first=False):
         def step(i, _):
             for u in range(UNROLL):
                 c = i * UNROLL + u
-                total = product(slots[0], c)
+                total = product(a_slot, b_slot, table, slots[0], c)
                 for slot in slots[1:]:
-                    total = total + product(slot, c)
+                    total = total + product(a_slot, b_slot, table, slot, c)
                 acc[c] = total if first else acc[c] + total
-            if last:
-                out_copy(i).start()
             return 0
 
         count = n_own // UNROLL // part[1]
         lax.fori_loop(part[0] * count, (part[0] + 1) * count, step, 0)
-
-    def out_copy(i):
-        where = pl.ds(i * UNROLL, UNROLL)
-        return pltpu.make_async_copy(acc.at[where], out_hbm.at[where], out_sem.at[i])
 
     def from_partner(dx):
         for move in moves:
             if move.link == "d" and move.dst == dx:
                 receive(move)
 
-    jobs = []
-    queued = set()
-    stage = 0
-
     def ready(dx):
         return not [s for s in steps if s[1] == "take" and s[2].dst == dx]
 
+    early = [dx for dx in range(n_x) if 2 * dx not in LATE]
+    jobs, queued = [], set()
+    stage, clock = 0, 0.0
     while steps:
         now = steps[0][0]
         if stage == 0 and now > TABLE_AT:
@@ -307,30 +298,66 @@
             stage = 1
         elif stage == 1 and now > TABLE_AT + 3.0:
             use_table()
-            from_partner(0)
-            jobs += [functools.partial(compute, (0, 1), (i, PIECES), first=True) for i in range(PIECES)]
             stage = 2
+        for dx in early:
+            if stage == 2 and dx not in queued and ready(dx):
+                jobs.append((0.0, functools.partial(from_partner, dx)))
+                jobs += [(JOB, functools.partial(compute, (2 * dx, 2 * dx + 1), (i, PIECES), first=not queued)) for i in range(PIECES)]
+                queued.add(dx)
+        clock = max(clock, now)
         run(steps.pop(0))
-        while steps and steps[0][1] == "send":
+        while steps and steps[0][0] == now:
             run(steps.pop(0))
-        for dx in (1, 3):
-            if dx not in queued and ready(dx):
-                queued.add(dx)
-                jobs.append(functools.partial(from_partner, dx))
-                jobs += [functools.partial(compute, (2 * dx, 2 * dx + 1), (i, PIECES)) for i in range(PIECES)]
-        if jobs:
-            jobs.pop(0)()
-    for job in jobs:
+        until = steps[0][0] if steps else clock + 100.0
+        while jobs and clock + jobs[0][0] < until + 1.0:
+            cost, job = jobs.pop(0)
+            job()
+            clock += cost
+    for _, job in jobs:
         job()
-    compute((4,))
-    from_partner(2)
-    compute((5,), last=True)
+    for dx in range(n_x):
+        if dx not in early:
+            from_partner(dx)
 
     for number, (dx, other) in enumerate(peers):
         for one in lists(number, dx, other):
             one.wait_send()
     for move in moves:
         copy(move, y).wait_send()
+
+
+def product(a_slot, b_slot, table, slot, c):
+    left = a_slot[slot][table[0, slot, c]]
+    right = b_slot[slot][table[1, slot, c]]
+    part = jnp.dot(left, right, preferred_element_type=jnp.float32)
+    return part.astype(jnp.bfloat16).astype(jnp.float32)
+
+
+def finish_kernel(acc, table_v, *refs):
+    a_slot = {slot: refs[2 * place] for place, slot in enumerate(LATE)}
+    b_slot = {slot: refs[2 * place + 1] for place, slot in enumerate(LATE)}
+    out_hbm, total_v, table, sem, out_sem = refs[2 * len(LATE):]
+    n_own = acc.shape[0]
+    to_smem = pltpu.make_async_copy(table_v, table, sem)
+    to_smem.start()
+    to_smem.wait()
+
+    def out_copy(i):
+        where = pl.ds(i * UNROLL, UNROLL)
+        return pltpu.make_async_copy(total_v.at[where], out_hbm.at[where], out_sem.at[i])
+
+    def step(i, _):
+        for u in range(UNROLL):
+            c = i * UNROLL + u
+            total = None if len(LATE) == 8 else acc[c]
+            for slot in LATE:
+                part = product(a_slot, b_slot, table, slot, c)
+                total = part if total is None else total + part
+            total_v[c] = total
+        out_copy(i).start()
+        return 0
+
+    lax.fori_loop(0, n_own // UNROLL, step, 0)
     for i in range(n_own // UNROLL):
         out_copy(i).wait()
 
@@ -350,33 +377,51 @@
         assert n_x == 4 and n_y == 4 and n_part == n_x * 128 and 128 % n_own == 0
         moves = plan(n_a, n_b)
         in_hbm = pl.BlockSpec(memory_space=pltpu.HBM)
-        out = pl.pallas_call(
-            functools.partial(kernel, (n_x, n_y, n_a, n_b, n_own)),
-            out_shape=jax.ShapeDtypeStruct((n_own, size, size), jnp.float32),
+        in_vmem = pl.BlockSpec(memory_space=pltpu.VMEM)
+        a_shape, b_shape = (n_a, size, size), (n_b, size, size)
+        operands = [
+            pltpu.with_memory_space_constraint(one, pltpu.HBM)
+            for one in (a, b, pair_loc[0, 0, :, 0, :].T, plist_loc[0, 0].T, cidx_loc[0, 0].T)
+        ]
+        state = pl.pallas_call(
+            functools.partial(gather_kernel, (n_x, n_y, n_a, n_b, n_own)),
+            name="gather",
+            out_shape=[pltpu.VMEM((n_own, size, size), jnp.float32), pltpu.VMEM((2, 8, 128), jnp.int32)]
+            + [pltpu.VMEM(a_shape, jnp.bfloat16), pltpu.VMEM(b_shape, jnp.bfloat16)] * len(LATE),
             in_specs=[in_hbm] * 5,
-            out_specs=in_hbm,
-            scratch_shapes=[pltpu.VMEM((n_a, size, size), jnp.bfloat16)] * 8
-            + [pltpu.VMEM((n_b, size, size), jnp.bfloat16)] * 8
+            out_specs=[in_vmem] * (2 + 2 * len(LATE)),
+            scratch_shapes=[pltpu.VMEM(a_shape, jnp.bfloat16), pltpu.VMEM(b_shape, jnp.bfloat16)] * (8 - len(LATE))
             + [
-                pltpu.VMEM((n_own, size, size), jnp.float32),
                 pltpu.VMEM((2, n_part), jnp.int32),
                 pltpu.VMEM((2, n_part), jnp.int32),
                 pltpu.VMEM((2, n_own), jnp.int32),
                 pltpu.VMEM((8, 2, 128), jnp.int32),
                 pltpu.VMEM((8, 2, 128), jnp.int32),
-                pltpu.VMEM((2, 8, 128), jnp.int32),
                 pltpu.SMEM((2, 8, 128), jnp.int32),
                 pltpu.SemaphoreType.DMA((len(moves),)),
                 pltpu.SemaphoreType.DMA((len(moves),)),
                 pltpu.SemaphoreType.DMA((14,)),
                 pltpu.SemaphoreType.DMA((14,)),
                 pltpu.SemaphoreType.DMA((6,)),
+            ],
+            compiler_params=pltpu.CompilerParams(
+                collective_id=0, has_side_effects=True, vmem_limit_bytes=28 * 1024 * 1024
+            ),
+        )(*operands)
+        out = pl.pallas_call(
+            finish_kernel,
+            name="finish",
+            out_shape=jax.ShapeDtypeStruct((n_own, size, size), jnp.float32),
+            in_specs=[in_vmem] * len(state),
+            out_specs=in_hbm,
+            scratch_shapes=[
+                pltpu.VMEM((n_own, size, size), jnp.float32),
+                pltpu.SMEM((2, 8, 128), jnp.int32),
+                pltpu.SemaphoreType.DMA,
                 pltpu.SemaphoreType.DMA((n_own // UNROLL,)),
             ],
-            compiler_params=pltpu.CompilerParams(
-                collective_id=0, has_side_effects=True, vmem_limit_bytes=VMEM
-            ),
-        )(a, b, pair_loc[0, 0, :, 0, :].T, plist_loc[0, 0].T, cidx_loc[0, 0].T)
+            compiler_params=pltpu.CompilerParams(vmem_limit_bytes=28 * 1024 * 1024),
+        )(*state)
         return out[None, None]
 
     return jax.shard_map(

time: 73.1 us -> 68.3 us (0.934)
  local copies, waits for them, and re-layouts: 4.7 us -> 0 us
    unnamed x1 -> x0, local copies, waits for them, and re-layouts: 4.7 us -> none
    pallas_call x1 -> x2, Pallas kernels: 68.2 us -> 68.2 us  [the longest x1 64.3 us: device_step(): pl.pallas_call(functools.partial(gather_kernel, (n_x, n_y, n_a, n_b, n_ow...]
where the time goes in v8:
time: 68.3 us; the launch traced here: 68.2 us
  Pallas kernels  68.2 us (100%)
    pallas_call x1, Pallas kernels, device_step(): pl.pallas_call(functools.partial(gather_kernel, (n_x, n_y, n_a, n_b, n_ow...  64.3 us
    pallas_call x1, Pallas kernels, device_step(): pl.pallas_call(finish_kernel, name='finish', out_shape=jax.ShapeDtypeStru...  3.95 us

profile of v8, /device:TPU:97, one launch (start us, length us, event | category | flops | bytes accessed | tf_op | source)
XLA Modules:
  0.0 68.2 jit_solution(6623273656475759854)
XLA Ops:
  0.0 64.3 %gather.1 = (f32[64,128,128]{2,1,0:T(8,128)S(1)}, s32[2,8,128]{2,1,0:T(8,128)S(1)}, bf16[16,128,128]{2,1,0:T(8,128)(2,1)S(1)}, bf16[64,128,128]{2,1,0:T(8,128)(2...) custom-call(bf16[16,128,128]{2,1,0:T(8,128)(2,1)} %bitcast.13, ...), custom_call_target="tpu_custom_call" | custom-call | tf_op jit(solution)/shard_map/gather/pallas_call | solution.py:386
  64.3 3.9 %finish.1 = f32[64,128,128]{2,1,0:T(8,128)} custom-call(f32[64,128,128]{2,1,0:T(8,128)S(1)} %get-tuple-element.11.acc, s32[2,8,128]{2,1,0:T(8,128)S(1)} %get-tuple-element.12.table_v, bf16[16,128,128]{2,1,0:T(8,128)(2,1)S(1)} %get-tuple-element.13.refs_0_, bf16[64,128,128]{2,1,0:T(8,128)(2,1)S(1)} %get-tuple-element.14.refs_1_, ...), custom_call_target="tpu_custom_call" | custom-call | tf_op jit(solution)/shard_map/finish/pallas_call | solution.py:411

commit v9 on v8

--- a/solution.py
+++ b/solution.py
@@ -8,11 +8,13 @@
 from jax.sharding import PartitionSpec as P
 
 MESH = pl.DeviceIdType.MESH
-HALF_SET = 40
-CHUNK = 5
+HALF_SET = 48
+CHUNK = 4
 A_CHUNK = 4
-WINDOW = 6
-TABLE_AT = 6.0
+A_GATE = 0
+B_GATE = 0
+SLACK = 2.0
+FEED_SLACK = 1.0
 VMEM = 67_000_000
 LAG = 3.0
 LATE = (4, 5)
@@ -64,8 +66,9 @@
         else:
             add("-y", "b", move.dst, move.dst, "q", piece, down, far + 2, 1)
 
-    for kind, count in (("b", n_b), ("a", n_a)):
+    for kind, count in (("b", n_b), ("a", n_a), ("l", 1)):
         add("d", kind, 0, 0, "all", (0, count), None, 9)
+    listed = set()
     for link, slot in (("+x", 3), ("-x", 1)):
         first = link == "+x"
         for part, one, two in (("q", q1, q2), ("h", h1, h2)):
@@ -75,9 +78,16 @@
                 spread(move, piece, 0)
                 if piece in keep:
                     spread(add(link, "b", slot, 2, part, piece, move, 1), piece, 3)
+                if slot not in listed:
+                    listed.add(slot)
+                    lists = add(link, "l", 0, slot, "all", (0, 1), None, 0)
+                    if first:
+                        add(link, "l", slot, 2, "all", (0, 1), lists, 1)
         keep = a1 if first else a2
+        mine = [m for m in moves if m.link == link and m.src == 0 and m.kind == "b"]
+        gate = mine[-1 - (A_GATE if first else B_GATE)]
         for piece in (a1 + a2) if first else (a2 + a1):
-            move = add(link, "a", 0, slot, "all", piece, None, 2)
+            move = add(link, "a", 0, slot, "all", piece, gate, 2)
             if piece in keep:
                 add(link, "a", slot, 2, "all", piece, move, 3)
     return moves
@@ -86,40 +96,32 @@
 LINKS = ("+x", "-x", "+y", "-y")
 
 
+def slack(move):
+    feeds = [m for m in move.after if m.link != "d"]
+    if move.link in ("+x", "-x"):
+        return 0.0 if feeds else SLACK
+    return FEED_SLACK if feeds else SLACK
+
+
 def order(moves):
-    waiting = {link: [m for m in moves if m.link == link and m.dep is None] for link in LINKS}
-    flying = {link: 0 for link in LINKS}
     free = {link: 0.0 for link in LINKS}
     events, steps, now = [], [], 0.0
 
-    def send():
-        for link in LINKS:
-            waiting[link].sort(key=lambda m: (m.rank, m.index))
-        busy = True
-        while busy:
-            busy = False
-            for link in LINKS:
-                if waiting[link] and flying[link] < WINDOW:
-                    move = waiting[link].pop(0)
-                    flying[link] += 1
-                    free[link] = max(now, free[link]) + move.count
-                    events.append((free[link] + LAG, move.index, move))
-                    steps.append((now, "send", move))
-                    busy = True
-
-    send()
+    def send(move):
+        steps.append((now, "send", move))
+        if move.link != "d":
+            free[move.link] = max(now, free[move.link]) + (0.3 if move.kind == "l" else move.count)
+            events.append((free[move.link] + LAG + slack(move), move.index, move))
+
+    for move in moves:
+        if move.dep is None and move.link != "d":
+            send(move)
     while events:
         events.sort(key=lambda e: e[:2])
         now, _, move = events.pop(0)
-        flying[move.link] -= 1
         steps.append((now, "take", move))
-        for nxt in move.after:
-            if nxt.link == "d":
-                steps.append((now, "send", nxt))
-            else:
-                waiting[nxt.link].append(nxt)
-        send()
-    assert not any(waiting.values())
+        for nxt in sorted(move.after, key=lambda m: (m.link == "d", m.rank)):
+            send(nxt)
     return steps
 
 
@@ -128,8 +130,8 @@
     a_slot, b_slot = list(refs[0:8]), list(refs[8:16])
     for place, slot in enumerate(LATE + tuple(s for s in range(8) if s not in LATE)):
         a_slot[slot], b_slot[slot] = refs[2 * place], refs[2 * place + 1]
-    (pairs_own, plist_own, own, pairs_in, plist_in, table,
-     send_sem, recv_sem, list_send, list_recv, load_sem) = refs[16:]
+    l_slot = refs[16:24]
+    own, table, send_sem, recv_sem, load_sem = refs[24:]
     y = lax.axis_index("rows")
     p = lax.axis_index("ksplit")
     x, core = p // 2, p % 2
@@ -150,20 +152,17 @@
     loads = [
         pltpu.make_async_copy(b_hbm, b_slot[0], load_sem.at[0]),
         pltpu.make_async_copy(a_hbm, a_slot[0], load_sem.at[1]),
-        pltpu.make_async_copy(pairs_hbm, pairs_own, load_sem.at[2]),
-        pltpu.make_async_copy(plist_hbm, plist_own, load_sem.at[3]),
+        pltpu.make_async_copy(pairs_hbm, l_slot[0].at[0], load_sem.at[2]),
+        pltpu.make_async_copy(plist_hbm, l_slot[0].at[1], load_sem.at[3]),
         pltpu.make_async_copy(own_hbm, own, load_sem.at[4]),
     ]
     for load in loads:
         load.start()
 
-    peers = [(dx, other) for dx in range(n_x) for other in range(2) if (dx, other) != (0, 0)]
     barrier = pltpu.get_barrier_semaphore()
-    for dx, other in peers:
-        pl.semaphore_signal(barrier, inc=1, device_id={"ksplit": at(dx, other)}, device_id_type=MESH)
-    for link in ("+y", "-y"):
-        pl.semaphore_signal(barrier, inc=1, device_id=target[link], device_id_type=MESH)
-    pl.semaphore_wait(barrier, len(peers) + 2)
+    for device in target.values():
+        pl.semaphore_signal(barrier, inc=1, device_id=device, device_id_type=MESH)
+    pl.semaphore_wait(barrier, len(target))
 
     def copy(move, row):
         holder = (row + move.shift + 2 * n_y) % n_y
@@ -171,12 +170,14 @@
         quarter = (n_b - HALF_SET) // 4
         base = {"all": 0, "h": (holder % 2) * half, "q": HALF_SET + holder * quarter}[move.part]
         where = pl.ds(base + move.first, move.count)
-        slots = a_slot if move.kind == "a" else b_slot
+        slots = {"a": a_slot, "b": b_slot, "l": l_slot}[move.kind]
         src = slots[2 * move.src]
         dst = slots[2 * move.dst + (1 if move.link == "d" else 0)]
+        if move.kind != "l":
+            src, dst = src.at[where], dst.at[where]
         return pltpu.make_async_remote_copy(
-            src_ref=src.at[where],
-            dst_ref=dst.at[where],
+            src_ref=src,
+            dst_ref=dst,
             send_sem=send_sem.at[move.index],
             recv_sem=recv_sem.at[move.index],
             device_id=target[move.link],
@@ -189,36 +190,6 @@
     def receive(move):
         row = {"+y": y + n_y - 1, "-y": y + 1}.get(move.link, y)
         copy(move, row).wait_recv()
-
-    def lists(number, dx, other):
-        mine, theirs = 2 * dx + other, 2 * ((n_x - dx) % n_x) + other
-        where = pl.ds(pl.multiple_of(((x + dx) % n_x) * 128, 128), 128)
-        pair = []
-        for which, (src, dst) in enumerate(((pairs_own, pairs_in), (plist_own, plist_in))):
-            pair.append(pltpu.make_async_remote_copy(
-                src_ref=src.at[:, where],
-                dst_ref=dst.at[theirs],
-                send_sem=list_send.at[2 * number + which],
-                recv_sem=list_recv.at[2 * number + which],
-                device_id={"ksplit": at(dx, other)},
-                device_id_type=MESH,
-            ))
-        return pair
-
-    def lists_in(number, dx, other):
-        mine = 2 * dx + other
-        pair = []
-        back = peers.index(((n_x - dx) % n_x, other))
-        for which, (src, dst) in enumerate(((pairs_own, pairs_in), (plist_own, plist_in))):
-            pair.append(pltpu.make_async_remote_copy(
-                src_ref=src.at[:, pl.ds(0, 128)],
-                dst_ref=dst.at[mine],
-                send_sem=list_send.at[2 * back + which],
-                recv_sem=list_recv.at[2 * back + which],
-                device_id={"ksplit": at(dx, other)},
-                device_id_type=MESH,
-            ))
-        return pair
 
     def run(step):
         _, what, move = step
@@ -227,12 +198,7 @@
         else:
             receive(move)
 
-    for load in loads[2:]:
-        load.wait()
-    for number, (dx, other) in enumerate(peers):
-        for one in lists(number, dx, other):
-            one.start()
-    for load in loads[:2]:
+    for load in loads:
         load.wait()
     while steps[0][1] == "send":
         run(steps.pop(0))
@@ -241,14 +207,14 @@
             start(move)
 
     def make_table():
+        for move in moves:
+            if move.kind == "l" and move.link == "d":
+                receive(move)
         mine = pl.ds(pl.multiple_of(x * 128, 128), 128)
-        pairs_in[0] = pairs_own[:, mine]
-        plist_in[0] = plist_own[:, mine]
-        for number, (dx, other) in enumerate(peers):
-            for one in lists_in(number, dx, other):
-                one.wait_recv()
-        key = plist_in[:, 0, :] * 65536 + plist_in[:, 1, :]
-        code = pairs_in[:, 0, :] * 65536 + pairs_in[:, 1, :]
+        rows = [[slot[what, which:which + 1, mine] for slot in l_slot] for what in range(2) for which in range(2)]
+        pair_a, pair_q, at_i, at_j = [jnp.concatenate(row, axis=0) for row in rows]
+        key = at_i * 65536 + at_j
+        code = pair_a * 65536 + pair_q
         wanted = own[0:1, :] * 65536 + own[1:2, :]
         wanted = jnp.concatenate([wanted] * (128 // n_own), axis=1)
         wanted = jnp.broadcast_to(wanted, key.shape)
@@ -282,7 +248,7 @@
 
     def from_partner(dx):
         for move in moves:
-            if move.link == "d" and move.dst == dx:
+            if move.link == "d" and move.dst == dx and move.kind != "l":
                 receive(move)
 
     def ready(dx):
@@ -291,12 +257,13 @@
     early = [dx for dx in range(n_x) if 2 * dx not in LATE]
     jobs, queued = [], set()
     stage, clock = 0, 0.0
+    listed = max(at for at, what, move in steps if what == "take" and move.kind == "l")
     while steps:
         now = steps[0][0]
-        if stage == 0 and now > TABLE_AT:
+        if stage == 0 and now > listed + 2.0:
             make_table()
             stage = 1
-        elif stage == 1 and now > TABLE_AT + 3.0:
+        elif stage == 1 and now > listed + 5.0:
             use_table()
             stage = 2
         for dx in early:
@@ -319,9 +286,6 @@
         if dx not in early:
             from_partner(dx)
 
-    for number, (dx, other) in enumerate(peers):
-        for one in lists(number, dx, other):
-            one.wait_send()
     for move in moves:
         copy(move, y).wait_send()
 
@@ -392,16 +356,13 @@
             out_specs=[in_vmem] * (2 + 2 * len(LATE)),
             scratch_shapes=[pltpu.VMEM(a_shape, jnp.bfloat16), pltpu.VMEM(b_shape, jnp.bfloat16)] * (8 - len(LATE))
             + [
-                pltpu.VMEM((2, n_part), jnp.int32),
-                pltpu.VMEM((2, n_part), jnp.int32),
+                pltpu.VMEM((2, 2, n_part), jnp.int32) for _ in range(8)
+            ]
+            + [
                 pltpu.VMEM((2, n_own), jnp.int32),
-                pltpu.VMEM((8, 2, 128), jnp.int32),
-                pltpu.VMEM((8, 2, 128), jnp.int32),
                 pltpu.SMEM((2, 8, 128), jnp.int32),
                 pltpu.SemaphoreType.DMA((len(moves),)),
                 pltpu.SemaphoreType.DMA((len(moves),)),
-                pltpu.SemaphoreType.DMA((14,)),
-                pltpu.SemaphoreType.DMA((14,)),
                 pltpu.SemaphoreType.DMA((6,)),
             ],
             compiler_params=pltpu.CompilerParams(

time: 68.3 us -> 67.5 us (0.988)
  Pallas kernels: 68.2 us -> 67.4 us
    pallas_call x1, Pallas kernels: 64.3 us -> 63.4 us  [device_step(): pl.pallas_call(functools.partial(gather_kernel, (n_x, n_y, n_a, n_b, n_ow...]
where the time goes in v9:
time: 67.5 us; the launch traced here: 67.4 us
  Pallas kernels  67.4 us (100%)
    pallas_call x1, Pallas kernels, device_step(): pl.pallas_call(functools.partial(gather_kernel, (n_x, n_y, n_a, n_b, n_ow...  63.4 us
    pallas_call x1, Pallas kernels, device_step(): pl.pallas_call(finish_kernel, name='finish', out_shape=jax.ShapeDtypeStru...  3.95 us

profile of v9, /device:TPU:97, one launch (start us, length us, event | category | flops | bytes accessed | tf_op | source)
XLA Modules:
  0.0 67.4 jit_solution(7657042714438833348)
XLA Ops:
  0.0 63.4 %gather.1 = (f32[64,128,128]{2,1,0:T(8,128)S(1)}, s32[2,8,128]{2,1,0:T(8,128)S(1)}, bf16[16,128,128]{2,1,0:T(8,128)(2,1)S(1)}, bf16[64,128,128]{2,1,0:T(8,128)(2...) custom-call(bf16[16,128,128]{2,1,0:T(8,128)(2,1)} %bitcast.13, ...), custom_call_target="tpu_custom_call" | custom-call | tf_op jit(solution)/shard_map/gather/pallas_call | solution.py:350
  63.4 3.9 %finish.1 = f32[64,128,128]{2,1,0:T(8,128)} custom-call(f32[64,128,128]{2,1,0:T(8,128)S(1)} %get-tuple-element.11.acc, s32[2,8,128]{2,1,0:T(8,128)S(1)} %get-tuple-element.12.table_v, bf16[16,128,128]{2,1,0:T(8,128)(2,1)S(1)} %get-tuple-element.13.refs_0_, bf16[64,128,128]{2,1,0:T(8,128)(2,1)S(1)} %get-tuple-element.14.refs_1_, ...), custom_call_target="tpu_custom_call" | custom-call | tf_op jit(solution)/shard_map/finish/pallas_call | solution.py:372

commit v10 on v9

--- a/solution.py
+++ b/solution.py
@@ -8,8 +8,8 @@
 from jax.sharding import PartitionSpec as P
 
 MESH = pl.DeviceIdType.MESH
-HALF_SET = 48
-CHUNK = 4
+HALF_SET = 40
+CHUNK = 5
 A_CHUNK = 4
 A_GATE = 0
 B_GATE = 0

time: 67.5 us -> 62.8 us (0.930)
  Pallas kernels: 67.4 us -> 62.7 us
    pallas_call x1, Pallas kernels: 63.4 us -> 58.7 us  [device_step(): pl.pallas_call(functools.partial(gather_kernel, (n_x, n_y, n_a, n_b, n_ow...]
where the time goes in v10:
time: 62.8 us; the launch traced here: 62.7 us
  Pallas kernels  62.7 us (100%)
    pallas_call x1, Pallas kernels, device_step(): pl.pallas_call(functools.partial(gather_kernel, (n_x, n_y, n_a, n_b, n_ow...  58.7 us
    pallas_call x1, Pallas kernels, device_step(): pl.pallas_call(finish_kernel, name='finish', out_shape=jax.ShapeDtypeStru...  3.96 us

profile of v10, /device:TPU:97, one launch (start us, length us, event | category | flops | bytes accessed | tf_op | source)
XLA Modules:
  0.0 62.7 jit_solution(964137726256292597)
XLA Ops:
  0.0 58.7 %gather.1 = (f32[64,128,128]{2,1,0:T(8,128)S(1)}, s32[2,8,128]{2,1,0:T(8,128)S(1)}, bf16[16,128,128]{2,1,0:T(8,128)(2,1)S(1)}, bf16[64,128,128]{2,1,0:T(8,128)(2...) custom-call(bf16[16,128,128]{2,1,0:T(8,128)(2,1)} %bitcast.13, ...), custom_call_target="tpu_custom_call" | custom-call | tf_op jit(solution)/shard_map/gather/pallas_call | solution.py:350
  58.7 4.0 %finish.1 = f32[64,128,128]{2,1,0:T(8,128)} custom-call(f32[64,128,128]{2,1,0:T(8,128)S(1)} %get-tuple-element.11.acc, s32[2,8,128]{2,1,0:T(8,128)S(1)} %get-tuple-element.12.table_v, bf16[16,128,128]{2,1,0:T(8,128)(2,1)S(1)} %get-tuple-element.13.refs_0_, bf16[64,128,128]{2,1,0:T(8,128)(2,1)S(1)} %get-tuple-element.14.refs_1_, ...), custom_call_target="tpu_custom_call" | custom-call | tf_op jit(solution)/shard_map/finish/pallas_call | solution.py:372

commit v11 on v10

--- a/solution.py
+++ b/solution.py
@@ -8,7 +8,7 @@
 from jax.sharding import PartitionSpec as P
 
 MESH = pl.DeviceIdType.MESH
-HALF_SET = 40
+HALF_SET = 36
 CHUNK = 5
 A_CHUNK = 4
 A_GATE = 0

time: 62.8 us -> 62.5 us (level)
  no operation moved by 1% of the time
where the time goes in v11:
time: 62.5 us; the launch traced here: 62.4 us
  Pallas kernels  62.4 us (100%)
    pallas_call x1, Pallas kernels, device_step(): pl.pallas_call(functools.partial(gather_kernel, (n_x, n_y, n_a, n_b, n_ow...  58.4 us
    pallas_call x1, Pallas kernels, device_step(): pl.pallas_call(finish_kernel, name='finish', out_shape=jax.ShapeDtypeStru...  3.94 us

profile of v11, /device:TPU:97, one launch (start us, length us, event | category | flops | bytes accessed | tf_op | source)
XLA Modules:
  0.0 62.4 jit_solution(319924941911609136)
XLA Ops:
  0.0 58.4 %gather.1 = (f32[64,128,128]{2,1,0:T(8,128)S(1)}, s32[2,8,128]{2,1,0:T(8,128)S(1)}, bf16[16,128,128]{2,1,0:T(8,128)(2,1)S(1)}, bf16[64,128,128]{2,1,0:T(8,128)(2...) custom-call(bf16[16,128,128]{2,1,0:T(8,128)(2,1)} %bitcast.13, ...), custom_call_target="tpu_custom_call" | custom-call | tf_op jit(solution)/shard_map/gather/pallas_call | solution.py:350
  58.4 3.9 %finish.1 = f32[64,128,128]{2,1,0:T(8,128)} custom-call(f32[64,128,128]{2,1,0:T(8,128)S(1)} %get-tuple-element.11.acc, s32[2,8,128]{2,1,0:T(8,128)S(1)} %get-tuple-element.12.table_v, bf16[16,128,128]{2,1,0:T(8,128)(2,1)S(1)} %get-tuple-element.13.refs_0_, bf16[64,128,128]{2,1,0:T(8,128)(2,1)S(1)} %get-tuple-element.14.refs_1_, ...), custom_call_target="tpu_custom_call" | custom-call | tf_op jit(solution)/shard_map/finish/pallas_call | solution.py:372

commit v12 on v11

--- a/solution.py
+++ b/solution.py
@@ -17,7 +17,7 @@
 FEED_SLACK = 1.0
 VMEM = 67_000_000
 LAG = 3.0
-LATE = (4, 5)
+LATE = (2, 3, 4, 5, 6, 7)
 JOB = 0.8
 PIECES = 4
 UNROLL = 8

time: 62.5 us -> 63.9 us (1.022)
  Pallas kernels: 62.4 us -> 63.8 us
    pallas_call x1, Pallas kernels: 3.94 us -> 6.27 us  [device_step(): pl.pallas_call(finish_kernel, name='finish', out_shape=jax.ShapeDtypeStru...]
    pallas_call x1, Pallas kernels: 58.4 us -> 57.6 us  [device_step(): pl.pallas_call(functools.partial(gather_kernel, (n_x, n_y, n_a, n_b, n_ow...]
where the time goes in v12:
time: 63.9 us; the launch traced here: 63.8 us
  Pallas kernels  63.8 us (100%)
    pallas_call x1, Pallas kernels, device_step(): pl.pallas_call(functools.partial(gather_kernel, (n_x, n_y, n_a, n_b, n_ow...  57.6 us
    pallas_call x1, Pallas kernels, device_step(): pl.pallas_call(finish_kernel, name='finish', out_shape=jax.ShapeDtypeStru...  6.27 us

profile of v12, /device:TPU:97, one launch (start us, length us, event | category | flops | bytes accessed | tf_op | source)
XLA Modules:
  0.0 63.8 jit_solution(14004239127292899875)
XLA Ops:
  0.0 57.6 %gather.1 = (f32[64,128,128]{2,1,0:T(8,128)S(1)}, s32[2,8,128]{2,1,0:T(8,128)S(1)}, bf16[16,128,128]{2,1,0:T(8,128)(2,1)S(1)}, bf16[64,128,128]{2,1,0:T(8,128)(2...) custom-call(bf16[16,128,128]{2,1,0:T(8,128)(2,1)} %bitcast.13, ...), custom_call_target="tpu_custom_call" | custom-call | tf_op jit(solution)/shard_map/gather/pallas_call | solution.py:350
  57.6 6.3 %finish.1 = f32[64,128,128]{2,1,0:T(8,128)} custom-call(f32[64,128,128]{2,1,0:T(8,128)S(1)} %get-tuple-element.19.acc, s32[2,8,128]{2,1,0:T(8,128)S(1)} %get-tuple-element.20.table_v, bf16[16,128,128]{2,1,0:T(8,128)(2,1)S(1)} %get-tuple-element.21.refs_0_, bf16[64,128,128]{2,1,0:T(8,128)(2,1)S(1)} %get-tuple-element.22.refs_1_, ...), custom_call_target="tpu_custom_call" | custom-call | tf_op jit(solution)/shard_map/finish/pallas_call | solution.py:372

commit v13 on v11

--- a/solution.py
+++ b/solution.py
@@ -12,7 +12,7 @@
 CHUNK = 5
 A_CHUNK = 4
 A_GATE = 0
-B_GATE = 0
+B_GATE = 3
 SLACK = 2.0
 FEED_SLACK = 1.0
 VMEM = 67_000_000

time: 62.5 us -> 62.3 us (level)
  no operation moved by 1% of the time
where the time goes in v13:
time: 62.3 us; the launch traced here: 62.2 us
  Pallas kernels  62.2 us (100%)
    pallas_call x1, Pallas kernels, device_step(): pl.pallas_call(functools.partial(gather_kernel, (n_x, n_y, n_a, n_b, n_ow...  58.3 us
    pallas_call x1, Pallas kernels, device_step(): pl.pallas_call(finish_kernel, name='finish', out_shape=jax.ShapeDtypeStru...  3.94 us

profile of v13, /device:TPU:97, one launch (start us, length us, event | category | flops | bytes accessed | tf_op | source)
XLA Modules:
  0.0 62.2 jit_solution(10007420784912269901)
XLA Ops:
  0.0 58.3 %gather.1 = (f32[64,128,128]{2,1,0:T(8,128)S(1)}, s32[2,8,128]{2,1,0:T(8,128)S(1)}, bf16[16,128,128]{2,1,0:T(8,128)(2,1)S(1)}, bf16[64,128,128]{2,1,0:T(8,128)(2...) custom-call(bf16[16,128,128]{2,1,0:T(8,128)(2,1)} %bitcast.13, ...), custom_call_target="tpu_custom_call" | custom-call | tf_op jit(solution)/shard_map/gather/pallas_call | solution.py:350
  58.3 3.9 %finish.1 = f32[64,128,128]{2,1,0:T(8,128)} custom-call(f32[64,128,128]{2,1,0:T(8,128)S(1)} %get-tuple-element.11.acc, s32[2,8,128]{2,1,0:T(8,128)S(1)} %get-tuple-element.12.table_v, bf16[16,128,128]{2,1,0:T(8,128)(2,1)S(1)} %get-tuple-element.13.refs_0_, bf16[64,128,128]{2,1,0:T(8,128)(2,1)S(1)} %get-tuple-element.14.refs_1_, ...), custom_call_target="tpu_custom_call" | custom-call | tf_op jit(solution)/shard_map/finish/pallas_call | solution.py:372

commit v14 on v13

--- a/solution.py
+++ b/solution.py
@@ -17,6 +17,7 @@
 FEED_SLACK = 1.0
 VMEM = 67_000_000
 LAG = 3.0
+SHARE_AT = 12.0
 LATE = (4, 5)
 JOB = 0.8
 PIECES = 4
@@ -202,9 +203,6 @@
         load.wait()
     while steps[0][1] == "send":
         run(steps.pop(0))
-    for move in moves:
-        if move.dep is None and move.link == "d":
-            start(move)
 
     def make_table():
         for move in moves:
@@ -256,10 +254,15 @@
 
     early = [dx for dx in range(n_x) if 2 * dx not in LATE]
     jobs, queued = [], set()
-    stage, clock = 0, 0.0
+    stage, clock, shared = 0, 0.0, False
     listed = max(at for at, what, move in steps if what == "take" and move.kind == "l")
     while steps:
         now = steps[0][0]
+        if not shared and now > SHARE_AT:
+            shared = True
+            for move in moves:
+                if move.dep is None and move.link == "d":
+                    start(move)
         if stage == 0 and now > listed + 2.0:
             make_table()
             stage = 1

time: 62.3 us -> 62.3 us (level)
  no operation moved by 1% of the time
where the time goes in v14:
time: 62.3 us; the launch traced here: 62.2 us
  Pallas kernels  62.2 us (100%)
    pallas_call x1, Pallas kernels, device_step(): pl.pallas_call(functools.partial(gather_kernel, (n_x, n_y, n_a, n_b, n_ow...  58.3 us
    pallas_call x1, Pallas kernels, device_step(): pl.pallas_call(finish_kernel, name='finish', out_shape=jax.ShapeDtypeStru...  3.94 us

profile of v14, /device:TPU:97, one launch (start us, length us, event | category | flops | bytes accessed | tf_op | source)
XLA Modules:
  0.0 62.2 jit_solution(5271259339068084473)
XLA Ops:
  0.0 58.3 %gather.1 = (f32[64,128,128]{2,1,0:T(8,128)S(1)}, s32[2,8,128]{2,1,0:T(8,128)S(1)}, bf16[16,128,128]{2,1,0:T(8,128)(2,1)S(1)}, bf16[64,128,128]{2,1,0:T(8,128)(2...) custom-call(bf16[16,128,128]{2,1,0:T(8,128)(2,1)} %bitcast.13, ...), custom_call_target="tpu_custom_call" | custom-call | tf_op jit(solution)/shard_map/gather/pallas_call | solution.py:353
  58.3 3.9 %finish.1 = f32[64,128,128]{2,1,0:T(8,128)} custom-call(f32[64,128,128]{2,1,0:T(8,128)S(1)} %get-tuple-element.11.acc, s32[2,8,128]{2,1,0:T(8,128)S(1)} %get-tuple-element.12.table_v, bf16[16,128,128]{2,1,0:T(8,128)(2,1)S(1)} %get-tuple-element.13.refs_0_, bf16[64,128,128]{2,1,0:T(8,128)(2,1)S(1)} %get-tuple-element.14.refs_1_, ...), custom_call_target="tpu_custom_call" | custom-call | tf_op jit(solution)/shard_map/finish/pallas_call | solution.py:375
